TPU v7x, 256 devices: a whole 4x4x8 slice. The times are simulated.
256 devices in a mesh: freq: 8 (over z_lo, x), panel: 32 (over z_hi, y, core).
Axes of the slice: x: 4, y: 4, z: 8 (z_hi: 4, z_lo: 2; z = z_hi * 2 + z_lo), core: 2. Of those that a mesh axis runs over, the one named last changes fastest.
Arguments:
- recorded: float32 [8, 2, 2048, 2048], P('freq', None, 'panel'), parts along dimension 0, may hold values from -60 to 60
- receiver_kernel: bfloat16 [8, 2, 4095], P('freq'), parts along dimension 0, may hold values from -1.5 to 1.5
- source_kernel: bfloat16 [8, 2, 4095], P('freq'), parts along dimension 0, may hold values from -1.5 to 1.5
Outputs:
- primaries: float32 [8, 2, 2048, 2048], P('freq', None, 'panel'), parts along dimension 0
- multiples: bfloat16 [8, 2, 2048, 2048], P('freq', None, 'panel'), parts along dimension 0
There are 8 independent parts, one for each index of `freq`. A program takes and returns all parts, laid end to end along the dimension named above; each array names one. Nothing has to cross between parts.
All inputs are finite; a program needn't handle non-finite values.
Results may differ from a plain program's by a relative error of at most 0.0057.
Values may be sent and summed in bfloat16 or wider, within the bound.
A program may use at most 320 MiB of HBM per device.

v0:
```python
import jax
import jax.numpy as jnp
from jax import lax
from jax.sharding import PartitionSpec as P


def from_everyone(value, axis):
    copies = jnp.broadcast_to(value, (lax.axis_size(axis), *value.shape))
    return lax.all_to_all(copies, axis, split_axis=0, concat_axis=0, tiled=True)


def over_copies(value, axis):
    everything = from_everyone(value, axis)
    return jnp.sum(everything, axis=0)


def packed_total(arrays, axis):
    flat, at, outs = (jnp.concatenate([a.reshape(-1) for a in arrays]), 0, [])
    running = over_copies(flat, axis)
    for a in arrays:
        outs.append(running[at : at + a.size].reshape(a.shape))
        at += a.size
    return tuple(outs)


def band(kernel, base, nrows, ncols):
    length = nrows + ncols - 1
    piece = lax.dynamic_slice_in_dim(kernel, base - nrows + 1, length, 1)
    rolled = jnp.roll(piece, -(nrows - 1), axis=1)
    flat = jnp.tile(rolled, (1, nrows))[:, : nrows * (length - 1)]
    return flat.reshape(2, nrows, length - 1)[:, :, :ncols]


def complex_dot(left, right):
    real_part = jnp.dot(left[0], right[0], preferred_element_type=jnp.float32) - jnp.dot(
        left[1], right[1], preferred_element_type=jnp.float32
    )
    imag_part = jnp.dot(left[0], right[1], preferred_element_type=jnp.float32) + jnp.dot(
        left[1], right[0], preferred_element_type=jnp.float32
    )
    return jnp.stack([real_part, imag_part])


def per_device(recorded, receiver_kernel, source_kernel):
    freqs, rows, width = (recorded.shape[0], recorded.shape[2], recorded.shape[3])
    panels = lax.axis_size("panel")
    sources = rows * panels
    data_b = recorded.astype(jnp.bfloat16)
    focused = jnp.stack(
        [complex_dot(data_b[0], band(receiver_kernel[0], width - 1, width, width))]
    ).astype(jnp.bfloat16)
    row_first = lax.axis_index("panel") * rows
    local_oper = jnp.stack([band(source_kernel[0], sources - 1 - row_first, rows, sources)])
    oper = local_oper[0]
    parts = [complex_dot(oper, lax.all_gather(focused, "panel", axis=2, tiled=True)[0])]
    summed = jnp.stack(parts)
    mult = summed.astype(jnp.bfloat16)
    mfl = mult.astype(jnp.float32)
    num_re = jnp.sum(mfl[:, 0] * recorded[:, 0] + mfl[:, 1] * recorded[:, 1], axis=(1, 2))
    num_im = jnp.sum(mfl[:, 0] * recorded[:, 1] - mfl[:, 1] * recorded[:, 0], axis=(1, 2))
    energy = jnp.sum(mfl[:, 0] * mfl[:, 0] + mfl[:, 1] * mfl[:, 1], axis=(1, 2))
    num_re, num_im, energy = packed_total((num_re, num_im, energy), "panel")
    den = energy + 1e-06
    fit_re = (num_re / den)[:, None, None]
    fit_im = (num_im / den)[:, None, None]
    prim_re = recorded[:, 0] - (fit_re * mfl[:, 0] - fit_im * mfl[:, 1])
    prim_im = recorded[:, 1] - (fit_re * mfl[:, 1] + fit_im * mfl[:, 0])
    return (jnp.stack([prim_re, prim_im], axis=1), mult)


def solution(mesh):
    placed = (P("freq", None, "panel", None), P("freq", None, None), P("freq", None, None))
    return jax.shard_map(
        per_device,
        mesh=mesh,
        in_specs=placed,
        out_specs=(P("freq", None, "panel", None), P("freq", None, "panel", None)),
        check_vma=False,
    )
```

profile of v0, /device:TPU:1, one launch (start us, length us, event | category | flops | bytes accessed | tf_op | source)
XLA Modules:
  0.0 450.9 jit_solution(5513023352090350222)
XLA Ops:
  7.2 0.0 copy-start
  7.2 0.0 all-gather.2.cloned.1.call-start
  7.2 0.8 slice.125
  8.0 0.7 slice.126
  8.7 11.1 %tile.20 = bf16[2,2048,4095]{2,1,0:T(8,128)(2,1)} broadcast(bf16[2,4095]{1,0:T(2,128)(2,1)S(1)} %pad_maximum_fusion.3), dimensions={0,2} | broadcast | bytes 33562620 | tf_op jit(solution)/shard_map/tile | solution.py:30
  19.8 69.4 %reshape.275 = bf16[16773120]{0:T(1024)(128)(2,1)} reshape(bf16[2,2048,4095]{2,1,0:T(8,128)(2,1)} %tile.20) | data formatting | bytes 67092480
  89.2 39.9 %tile.21 = bf16[2,8386560]{1,0:T(2,128)(2,1)} reshape(bf16[16773120]{0:T(1024)(128)(2,1)} %reshape.275) | data formatting | bytes 67092480 | tf_op jit(solution)/shard_map/tile | solution.py:30
  129.2 27.0 %slice.127 = bf16[2,8384512]{1,0:T(2,128)(2,1)} slice(bf16[2,8386560]{1,0:T(2,128)(2,1)} %tile.21), slice={[0:2], [0:8384512]} | slice | bytes 67076096 | tf_op jit(solution)/shard_map/slice | solution.py:30
  156.2 52.8 %reshape.277 = bf16[16769024]{0:T(1024)(128)(2,1)} reshape(bf16[2,8384512]{1,0:T(2,128)(2,1)} %slice.127) | data formatting | bytes 67076096
  209.0 0.0 copy-start.1
  209.0 53.1 %reshape.274 = bf16[2,2048,4094]{2,1,0:T(8,128)(2,1)} reshape(bf16[16769024]{0:T(1024)(128)(2,1)} %reshape.277) | data formatting | bytes 67076096 | tf_op jit(solution)/shard_map/reshape | solution.py:31
  262.1 0.0 copy-done.1
  262.1 0.1 convert_element_type.36
  262.2 4.9 %fusion = f32[2048,64]{0,1:T(8,128)S(1)} fusion(bf16[2,2048,4094]{2,1,0:T(8,128)(2,1)} %reshape.274, bf16[1,2,64,2048]{3,2,1,0:T(8,128)(2,1)S(1)} %convert_element_type.36), kind=kOutput, calls=%fused_computation.4 | convolution fusion | flops 536870912 | bytes 9175040 | tf_op jit(solution)/shard_map/dot_general | solution.py:35
  267.1 4.9 %fusion.1 = f32[2048,64]{0,1:T(8,128)S(1)} fusion(bf16[2,2048,4094]{2,1,0:T(8,128)(2,1)} %reshape.274, bf16[1,2,64,2048]{3,2,1,0:T(8,128)(2,1)S(1)} %convert_element_type.36), kind=kOutput, calls=%fused_computation.5 | convolution fusion | flops 536870912 | bytes 9175040 | tf_op jit(solution)/shard_map/dot_general | solution.py:38
  272.1 5.0 %fusion.19 = bf16[1,1,64,2048]{3,2,1,0:T(8,128)(2,1)S(1)} fusion(f32[2048,64]{0,1:T(8,128)S(1)} %fusion, bf16[2,2048,4094]{2,1,0:T(8,128)(2,1)} %reshape.274, bf16[1,2,64,2048]{3,2,1,0:T(8,128)(2,1)S(1)} %convert_element_type.36), kind=kOutput, calls=%fused_computation.23 | convolution fusion | flops 537133056 | bytes 9437184 | tf_op jit(solution)/shard_map/dot_general | solution.py:35
  277.0 5.0 %fusion.18 = bf16[1,1,64,2048]{3,2,1,0:T(8,128)(2,1)S(1)} fusion(f32[2048,64]{0,1:T(8,128)S(1)} %fusion.1, bf16[2,2048,4094]{2,1,0:T(8,128)(2,1)} %reshape.274, bf16[1,2,64,2048]{3,2,1,0:T(8,128)(2,1)S(1)} %convert_element_type.36), kind=kOutput, calls=%fused_computation.22 | convolution fusion | flops 537133056 | bytes 9437184 | tf_op jit(solution)/shard_map/dot_general | solution.py:38
  282.0 0.8 pad_maximum_fusion.1
  282.8 0.0 all-gather.2.cloned.1.call-update
  282.8 0.0 copy-done
  282.9 0.1 dynamic-slice_bitcast_fusion
  282.9 0.1 slice.120
  283.1 0.9 tile.9
  284.0 0.6 slice.122
  284.7 1.5 reshape.273
  286.2 106.4 %all-gather.2.cloned.1.call-done = bf16[1,2,2048,2048]{3,2,1,0:T(8,128)(2,1)} async-done(((bf16[1,2,64,2048]{3,2,1,0:T(8,128)(2,1)}), bf16[1,2,2048,2048]{3,2,1,0:T(8,128)(2,1)}) %all-gather.2.cloned.1.call-update) | async-done | bytes 16777232 | tf_op jit(solution)/shard_map/all_gather | solution.py:55
  392.6 0.0 copy-start.2
  392.6 5.1 %fusion.5 = f32[64,2048]{1,0:T(8,128)S(1)} fusion(bf16[1,2,2048,2048]{3,2,1,0:T(8,128)(2,1)} %all-gather.2.cloned.1.call-done, bf16[2,64,2110]{2,1,0:T(8,128)(2,1)S(1)} %reshape.273), kind=kOutput, calls=%fused_computation.9 | convolution fusion | flops 536870912 | bytes 9175040 | tf_op jit(solution)/shard_map/dot_general | solution.py:35
  397.7 5.7 %fusion.4 = f32[64,2048]{1,0:T(8,128)S(1)} fusion(bf16[1,2,2048,2048]{3,2,1,0:T(8,128)(2,1)} %all-gather.2.cloned.1.call-done, bf16[2,64,2110]{2,1,0:T(8,128)(2,1)S(1)} %reshape.273), kind=kOutput, calls=%fused_computation.8 | convolution fusion | flops 536870912 | bytes 9175040 | tf_op jit(solution)/shard_map/dot_general | solution.py:38
  403.4 0.0 copy-done.2
  403.4 1.6 fusion.16
  405.0 1.6 fusion.17
  406.6 0.9 fusion.20
  407.4 0.9 add_reduce_fusion.1
  408.4 2.0 pad_maximum_fusion.5
  410.4 29.6 %all_to_all.6 = f32[32,1,3]{2,1,0:T(1,128)S(1)} all-to-all(f32[32,1,3]{2,1,0:T(1,128)S(1)} %broadcast_in_dim.2), channel_id=1, replica_groups=mesh['freq'=8,'panel'=32] {'panel'}, dimensions={0} | all-to-all | bytes 768 | tf_op jit(solution)/shard_map/all_to_all | solution.py:9
  440.0 0.1 reduce_sum.48
  440.0 0.7 fusion.21
  442.6 0.2 subtract_subtract_fusion
  442.8 1.0 pad_maximum_fusion
  (5 shorter events, 0.1 us)
Async XLA Ops:
  7.2 275.7 %copy-start = (bf16[1,2,4095]{2,1,0:T(2,128)(2,1)S(1)}, bf16[1,2,4095]{2,1,0:T(2,128)(2,1)}, u32[]{:S(2)}) copy-start(bf16[1,2,4095]{2,1,0:T(2,128)(2,1)} %param.5) | copy-start | bytes 49144
  7.2 385.4 %all-gather.2.cloned.1.call-start = ((), (), s32[]{:S(2)}) async-start(), calls=%async_computation.1 | async-start | bytes 17301504 | tf_op jit(solution)/shard_map/all_gather | solution.py:55
  209.0 53.1 %copy-start.1 = (f32[1,2,64,2048]{3,2,1,0:T(8,128)S(1)}, f32[1,2,64,2048]{3,2,1,0:T(8,128)}, u32[]{:S(2)}) copy-start(f32[1,2,64,2048]{3,2,1,0:T(8,128)} %param.3) | copy-start | bytes 3145732
  392.6 10.8 %copy-start.2 = (bf16[1,2,2048,2048]{3,2,1,0:T(8,128)(2,1)S(1)}, bf16[1,2,2048,2048]{3,2,1,0:T(8,128)(2,1)}, u32[]{:S(2)}) copy-start(bf16[1,2,2048,2048]{3,2,1,0:T(8,128)(2,1)} %all-gather.2.cloned.1.call-done) | copy-start | bytes 50331652
Sparse Core Ops, SparseCore 0:
  283.0 109.5 all-gather.1
where the time goes:
time: 459 us; the launch traced here: 451 us
  local copies, waits for them, and re-layouts  259 us (56%)
  waiting for transfers between devices  106 us (23%)
  matrix products  33.7 us (7%)
  blocking collectives  29.6 us (6%)
  between operations  16.3 us (4%)
  other arithmetic  6.01 us (1%)
    unnamed x8, local copies, waits for them, and re-layouts  122 us
    all_gather x1, waiting for transfers between devices, per_device(): lax.all_gather(focused, 'panel', axis=2, tiled=True)[0]  106 us
    reshape x2, local copies, waits for them, and re-layouts, band(): return flat.reshape(2, nrows, length - 1)[:, :, :ncols]  54.6 us
    another operation x4, local copies, waits for them, and re-layouts, band(): flat = jnp.tile(rolled, (1, nrows))[:, :nrows * (length - 1)]  52 us
    all_to_all x1, blocking collectives, from_everyone(): return lax.all_to_all(copies, axis, split_axis=0, concat_axis=0, tiled=True)  29.6 us
    slice x2, local copies, waits for them, and re-layouts, band(): flat = jnp.tile(rolled, (1, nrows))[:, :nrows * (length - 1)]  27.7 us
    dot_general x2, matrix products, complex_dot(): jnp.dot(left[1], right[0], preferred_element_type=jnp.float32)  10.6 us
    dot_general x2, matrix products, complex_dot(): jnp.dot(left[0], right[0], preferred_element_type=jnp.float32)  10 us
  transfers between devices with their start and end apart: 1, of which 1 were waited for; matrix products, arithmetic and copies ran while one was open for 1% of the time, Pallas kernels for 0%

commit v1 on v0

v1 whole, which is shorter than its diff:
```python
import functools

import jax
import jax.numpy as jnp
from jax import lax
from jax.experimental import pallas as pl
from jax.experimental.pallas import tpu as pltpu
from jax.sharding import PartitionSpec as P

MESH = pl.DeviceIdType.MESH
PANELS = 32
ROWS = 64
WIDTH = PANELS * ROWS
BLOCK = 256
BLOCKS = WIDTH // BLOCK
PER_BLOCK = BLOCK // ROWS
TAPS = 2 * WIDTH
UNITS = 2 * (2 * BLOCKS - 1)
PAIRS = PANELS // 2
STEP_OFFSETS = (4, 3, 5, 2, 6, 1, 7, 0)


def build_operator(taps_ref, oper_ref, index):
    row = taps_ref[pl.ds(index, 1), :]
    skew = pltpu.roll(jnp.broadcast_to(row, (8, TAPS)), 0, 1, stride=1, stride_axis=0)
    for e in range(8):
        low = pltpu.roll(skew, 16 * e + TAPS - 127, 1)
        high = pltpu.roll(skew, (16 * e + 8 + TAPS - 127) % TAPS, 1)
        rows = jnp.concatenate([low, high], axis=0).astype(jnp.bfloat16)
        for u in range(UNITS):
            at = 128 * (UNITS - 1 - u)
            oper_ref[index, 128 * u + 16 * e : 128 * u + 16 * e + 16, :] = rows[:, at : at + 256]


def kernel(
    rec_hbm,
    taps_ref,
    prim_hbm,
    mult_hbm,
    rec,
    oper,
    left,
    left_turned,
    send_a,
    got_a,
    send_b,
    got_b,
    mult,
    prim,
    part_out,
    part_in,
    local_sem,
    send_sem,
    recv_sem,
):
    me = lax.axis_index("panel")
    barrier = pltpu.get_barrier_semaphore()

    def greet(k, carry):
        pl.semaphore_signal(
            barrier, inc=1, device_id={"panel": lax.rem(me + k, PANELS)}, device_id_type=MESH
        )
        return carry

    lax.fori_loop(1, PANELS, greet, 0)
    load = pltpu.make_async_copy(rec_hbm.at[0], rec, local_sem.at[0])
    load.start()

    def build(index, carry):
        build_operator(taps_ref, oper, index)
        return carry

    def exchange(stage, src, dst, sender, receiver):
        return pltpu.make_async_remote_copy(
            src_ref=src.at[receiver],
            dst_ref=dst.at[sender],
            send_sem=send_sem.at[stage, receiver],
            recv_sem=recv_sem.at[stage, sender],
            device_id={"panel": receiver},
            device_id_type=MESH,
        )

    def product(block, first):
        at = pl.multiple_of((BLOCKS - 1 - block) * BLOCK, BLOCK)
        return jnp.dot(
            left[...], oper[first, pl.ds(at, WIDTH), :], preferred_element_type=jnp.float32
        ) + jnp.dot(
            left_turned[...], oper[first + 1, pl.ds(at, WIDTH), :], preferred_element_type=jnp.float32
        )

    def send_block(stage, src, dst, block):
        for h in range(PER_BLOCK):
            target = block * PER_BLOCK + h

            @pl.when(target != me)
            def _():
                exchange(stage, src, dst, me, target).start()

            @pl.when(target == me)
            def _():
                dst[me] = src[me]

    lax.fori_loop(0, 2, build, 0)
    load.wait()
    data_re = rec[0].astype(jnp.bfloat16)
    data_im = rec[1].astype(jnp.bfloat16)
    left[0:ROWS, :] = data_re
    left[ROWS : 2 * ROWS, :] = data_im
    left_turned[0:ROWS, :] = -data_im
    left_turned[ROWS : 2 * ROWS, :] = data_re
    lane = lax.broadcasted_iota(jnp.int32, (ROWS, 128), 1)
    low_half = lane < ROWS
    first_block = me // PER_BLOCK

    def block_of(step):
        half = (step + 1) // 2
        away = jnp.where(lax.rem(step, 2) == 0, BLOCKS // 2 + half, BLOCKS // 2 - half)
        return lax.rem(first_block + away, BLOCKS)

    def forward(step, carry):
        block = block_of(step)
        result = product(block, 0)

        for g in range(2):
            re = result[0:ROWS, 128 * g : 128 * g + 128]
            im = result[ROWS : 2 * ROWS, 128 * g : 128 * g + 128]
            even = jnp.where(low_half, re, pltpu.roll(im, ROWS, 1))
            odd = jnp.where(low_half, pltpu.roll(re, ROWS, 1), im)
            send_a[block * PER_BLOCK + 2 * g] = even.astype(jnp.bfloat16)
            send_a[block * PER_BLOCK + 2 * g + 1] = odd.astype(jnp.bfloat16)

        @pl.when(step == 0)
        def _():
            pl.semaphore_wait(barrier, PANELS - 1)

        send_block(0, send_a, got_a, block)
        return carry

    lax.fori_loop(0, BLOCKS, forward, 0)
    lax.fori_loop(2, 4, build, 0)

    def wait_received(stage, src, dst, sender):
        @pl.when(sender != me)
        def _():
            exchange(stage, src, dst, sender, me).wait_recv()

    def wait_sent(stage, src, dst):
        def one(k, carry):
            exchange(stage, src, dst, me, lax.rem(me + k, PANELS)).wait_send()
            return carry

        lax.fori_loop(1, PANELS, one, 0)

    def turn(pair, carry):
        wait_received(0, send_a, got_a, 2 * pair)
        wait_received(0, send_a, got_a, 2 * pair + 1)
        both = jnp.concatenate([got_a[2 * pair], got_a[2 * pair + 1]], axis=0)
        flipped = both.astype(jnp.float32).T
        at = pl.ds(pl.multiple_of(pair * 128, 128), 128)
        left[:, at] = flipped.astype(jnp.bfloat16)
        left_turned[0:ROWS, at] = (-flipped[ROWS : 2 * ROWS]).astype(jnp.bfloat16)
        left_turned[ROWS : 2 * ROWS, at] = flipped[0:ROWS].astype(jnp.bfloat16)
        return carry

    lax.fori_loop(0, PAIRS, turn, 0)

    def backward(step, carry):
        block = block_of(step)
        result = product(block, 2).T.astype(jnp.bfloat16)
        for h in range(PER_BLOCK):
            send_b[block * PER_BLOCK + h] = result[ROWS * h : ROWS * (h + 1)]
        send_block(1, send_b, got_b, block)
        return carry

    lax.fori_loop(0, BLOCKS, backward, 0)
    wait_sent(0, send_a, got_a)

    def fold(x):
        total = x[0:8]
        for k in range(1, ROWS // 8):
            total = total + x[8 * k : 8 * k + 8]
        return total

    def collect(pair, carry):
        num_re, num_im, energy = carry
        wait_received(1, send_b, got_b, 2 * pair)
        wait_received(1, send_b, got_b, 2 * pair + 1)
        even = got_b[2 * pair].astype(jnp.float32)
        odd = got_b[2 * pair + 1].astype(jnp.float32)
        re = jnp.where(low_half, even, pltpu.roll(odd, ROWS, 1))
        im = jnp.where(low_half, pltpu.roll(even, ROWS, 1), odd)
        at = pl.ds(pl.multiple_of(pair * 128, 128), 128)
        mult[0, :, at] = re.astype(jnp.bfloat16)
        mult[1, :, at] = im.astype(jnp.bfloat16)
        data_re = rec[0, :, at]
        data_im = rec[1, :, at]
        return (
            num_re + fold(re * data_re + im * data_im),
            num_im + fold(re * data_im - im * data_re),
            energy + fold(re * re + im * im),
        )

    zero = jnp.zeros((8, 128), jnp.float32)
    num_re, num_im, energy = lax.fori_loop(0, PAIRS, collect, (zero, zero, zero))
    part_out[0:8] = num_re
    part_out[8:16] = num_im
    part_out[16:24] = energy
    keep = pltpu.make_async_copy(mult, mult_hbm.at[0], local_sem.at[1])
    keep.start()

    def share(k, wait):
        target = lax.rem(me + k, PANELS)
        return pltpu.make_async_remote_copy(
            src_ref=part_out,
            dst_ref=part_in.at[me],
            send_sem=send_sem.at[2, target],
            recv_sem=recv_sem.at[2, me],
            device_id={"panel": target},
            device_id_type=MESH,
        )

    def share_start(k, carry):
        share(k, False).start()
        return carry

    lax.fori_loop(1, PANELS, share_start, 0)
    wait_sent(1, send_b, got_b)

    def gather(k, total):
        sender = lax.rem(me + k, PANELS)
        pltpu.make_async_remote_copy(
            src_ref=part_out,
            dst_ref=part_in.at[sender],
            send_sem=send_sem.at[2, me],
            recv_sem=recv_sem.at[2, sender],
            device_id={"panel": sender},
            device_id_type=MESH,
        ).wait_recv()
        return total + part_in[sender]

    total = lax.fori_loop(1, PANELS, gather, part_out[...])
    sums = [jnp.sum(total[8 * k : 8 * k + 8], keepdims=True) for k in range(3)]
    den = sums[2] + 1e-06
    fit_re = sums[0] / den
    fit_im = sums[1] / den

    def subtract(pair, carry):
        at = pl.ds(pl.multiple_of(pair * 128, 128), 128)
        re = mult[0, :, at].astype(jnp.float32)
        im = mult[1, :, at].astype(jnp.float32)
        prim[0, :, at] = rec[0, :, at] - (fit_re * re - fit_im * im)
        prim[1, :, at] = rec[1, :, at] - (fit_re * im + fit_im * re)
        return carry

    lax.fori_loop(0, PAIRS, subtract, 0)
    store = pltpu.make_async_copy(prim, prim_hbm.at[0], local_sem.at[2])
    store.start()

    def share_done(k, carry):
        share(k, True).wait_send()
        return carry

    lax.fori_loop(1, PANELS, share_done, 0)
    keep.wait()
    store.wait()


def per_device(recorded, receiver_kernel, source_kernel):
    taps = jnp.concatenate([receiver_kernel[0], jnp.flip(source_kernel[0], axis=1)], axis=0)
    taps = jnp.pad(taps.astype(jnp.float32), ((0, 4), (0, 1)))
    vmem = pltpu.VMEM
    return pl.pallas_call(
        kernel,
        out_shape=(
            jax.ShapeDtypeStruct((1, 2, ROWS, WIDTH), jnp.float32),
            jax.ShapeDtypeStruct((1, 2, ROWS, WIDTH), jnp.bfloat16),
        ),
        in_specs=[
            pl.BlockSpec(memory_space=pl.ANY),
            pl.BlockSpec(memory_space=pltpu.VMEM),
        ],
        out_specs=(
            pl.BlockSpec(memory_space=pl.ANY),
            pl.BlockSpec(memory_space=pl.ANY),
        ),
        scratch_shapes=[
            vmem((2, ROWS, WIDTH), jnp.float32),
            vmem((4, 128 * UNITS, BLOCK), jnp.bfloat16),
            vmem((2 * ROWS, WIDTH), jnp.bfloat16),
            vmem((2 * ROWS, WIDTH), jnp.bfloat16),
            vmem((PANELS, ROWS, 128), jnp.bfloat16),
            vmem((PANELS, ROWS, 128), jnp.bfloat16),
            vmem((PANELS, ROWS, 128), jnp.bfloat16),
            vmem((PANELS, ROWS, 128), jnp.bfloat16),
            vmem((2, ROWS, WIDTH), jnp.bfloat16),
            vmem((2, ROWS, WIDTH), jnp.float32),
            vmem((24, 128), jnp.float32),
            vmem((PANELS, 24, 128), jnp.float32),
            pltpu.SemaphoreType.DMA((3,)),
            pltpu.SemaphoreType.DMA((3, PANELS)),
            pltpu.SemaphoreType.DMA((3, PANELS)),
        ],
        compiler_params=pltpu.CompilerParams(
            collective_id=0, has_side_effects=True, vmem_limit_bytes=48 * 1024 * 1024
        ),
    )(recorded, taps)


def solution(mesh):
    placed = (P("freq", None, "panel", None), P("freq", None, None), P("freq", None, None))
    return jax.shard_map(
        per_device,
        mesh=mesh,
        in_specs=placed,
        out_specs=(P("freq", None, "panel", None), P("freq", None, "panel", None)),
        check_vma=False,
    )
```

time: 459 us -> 72.7 us (0.16); the launches traced: 451 us -> 71.5 us
  local copies, waits for them, and re-layouts: 259 us -> 15.7 us
  waiting for transfers between devices: 106 us -> 0 us
  Pallas kernels: 0 us -> 55.1 us
  matrix products: 33.7 us -> 0 us
  blocking collectives: 29.6 us -> 0 us
  between operations: 16.3 us -> 0.66 us
  other arithmetic: 6.01 us -> 0.05 us
    unnamed x8, local copies, waits for them, and re-layouts: 122 us -> 15.7 us
    all_gather x1 -> x0, waiting for transfers between devices: 106 us -> none  [per_device(): lax.all_gather(focused, 'panel', axis=2, tiled=True)[0]]
    pallas_call x0 -> x1, Pallas kernels: none -> 55.1 us  [per_device(): pl.pallas_call(kernel, out_shape=(jax.ShapeDtypeStruct((1, 2, ROWS, WIDTH...]
    reshape x2 -> x0, local copies, waits for them, and re-layouts: 54.6 us -> none  [band(): return flat.reshape(2, nrows, length - 1)[:, :, :ncols]]
    another operation x4 -> x0, local copies, waits for them, and re-layouts: 52 us -> none  [band(): flat = jnp.tile(rolled, (1, nrows))[:, :nrows * (length - 1)]]
    dot_general x8 -> x0, matrix products: 33.7 us -> none  [the longest x2 10.6 us: complex_dot(): jnp.dot(left[1], right[0], preferred_element_type=jnp.float32)]
    slice x7 -> x0, local copies, waits for them, and re-layouts: 29.9 us -> none  [the longest x2 27.7 us: band(): flat = jnp.tile(rolled, (1, nrows))[:, :nrows * (length - 1)]]
    all_to_all x1 -> x0, blocking collectives: 29.6 us -> none  [from_everyone(): return lax.all_to_all(copies, axis, split_axis=0, concat_axis=0, tiled=True)]
  transfers between devices with their start and end apart: 1 -> 0, of which waited for: 1 -> 0; matrix products, arithmetic and copies ran while one was open for 1% -> 0% of each run, Pallas kernels for 0% -> 0%
where the time goes in v1:
time: 72.7 us; the launch traced here: 71.5 us
  Pallas kernels  55.1 us (76%)
  local copies, waits for them, and re-layouts  15.7 us (22%)
    pallas_call x1, Pallas kernels, per_device(): pl.pallas_call(kernel, out_shape=(jax.ShapeDtypeStruct((1, 2, ROWS, WIDTH...  55.1 us
    unnamed x8, local copies, waits for them, and re-layouts  15.7 us

profile of v1, /device:TPU:1, one launch (start us, length us, event | category | flops | bytes accessed | tf_op | source)
XLA Modules:
  0.0 71.5 jit_solution(3696231934980226736)
XLA Ops:
  0.6 12.0 %reverse = bf16[2,4096]{1,0:T(2,128)(2,1)S(1)} reverse(bf16[2,4096]{1,0:T(2,128)(2,1)} %bitcast.4), dimensions={1} | reverse | bytes 32768
  12.6 0.0 copy-start.1
  12.6 0.1 slice
  12.7 0.6 copy-done.1
  13.3 0.1 fusion.6.taps_ref
  13.4 0.0 copy-start
  13.4 1.2 %copy-done = f32[1,2,64,2048]{3,2,1,0:T(8,128)S(1)} copy-done((f32[1,2,64,2048]{3,2,1,0:T(8,128)S(1)}, f32[1,2,64,2048]{3,2,1,0:T(8,128)}, u32[]{:S(2)}) %copy-start) | copy-done | bytes 1048600
  14.6 55.1 %shard_map.50 = (f32[1,2,64,2048]{3,2,1,0:T(8,128)S(1)}, bf16[1,2,64,2048]{3,2,1,0:T(8,128)(2,1)S(1)}) custom-call(f32[1,2,64,2048]{3,2,1,0:T(8,128)S(1)} %copy-done, f32[8,4096]{1,0:T(8,128)S(1)} %fusion.6.taps_ref), custom_call_target="tpu_custom_call" | custom-call | tf_op jit(solution)/shard_map/pallas_call | solution.py:272
  69.7 1.0 %copy.7 = f32[1,2,64,2048]{3,2,1,0:T(8,128)} copy(f32[1,2,64,2048]{3,2,1,0:T(8,128)S(1)} %get-tuple-element.4) | data formatting | bytes 2097152
  70.7 0.8 %copy.8 = bf16[1,2,64,2048]{3,2,1,0:T(8,128)(2,1)} copy(bf16[1,2,64,2048]{3,2,1,0:T(8,128)(2,1)S(1)} %get-tuple-element.5) | data formatting | bytes 1048576
Async XLA Ops:
  12.6 0.7 %copy-start.1 = (bf16[1,2,4095]{2,1,0:T(2,128)(2,1)S(1)}, bf16[1,2,4095]{2,1,0:T(2,128)(2,1)}, u32[]{:S(2)}) copy-start(bf16[1,2,4095]{2,1,0:T(2,128)(2,1)} %param.4) | copy-start | bytes 49144
  13.4 1.2 %copy-start = (f32[1,2,64,2048]{3,2,1,0:T(8,128)S(1)}, f32[1,2,64,2048]{3,2,1,0:T(8,128)}, u32[]{:S(2)}) copy-start(f32[1,2,64,2048]{3,2,1,0:T(8,128)} %rec_hbm.1) | copy-start | bytes 3145732

commit v2 on v1

--- a/solution.py
+++ b/solution.py
@@ -17,15 +17,14 @@
 TAPS = 2 * WIDTH
 UNITS = 2 * (2 * BLOCKS - 1)
 PAIRS = PANELS // 2
-STEP_OFFSETS = (4, 3, 5, 2, 6, 1, 7, 0)
 
 
 def build_operator(taps_ref, oper_ref, index):
     row = taps_ref[pl.ds(index, 1), :]
     skew = pltpu.roll(jnp.broadcast_to(row, (8, TAPS)), 0, 1, stride=1, stride_axis=0)
     for e in range(8):
-        low = pltpu.roll(skew, 16 * e + TAPS - 127, 1)
-        high = pltpu.roll(skew, (16 * e + 8 + TAPS - 127) % TAPS, 1)
+        low = pltpu.roll(skew, 16 * e + TAPS - 128, 1)
+        high = pltpu.roll(skew, 16 * e + 8 + TAPS - 128, 1)
         rows = jnp.concatenate([low, high], axis=0).astype(jnp.bfloat16)
         for u in range(UNITS):
             at = 128 * (UNITS - 1 - u)
@@ -34,10 +33,13 @@
 
 def kernel(
     rec_hbm,
+    receiver_hbm,
+    source_hbm,
+    prim,
+    mult,
+    rec,
+    raw,
     taps_ref,
-    prim_hbm,
-    mult_hbm,
-    rec,
     oper,
     left,
     left_turned,
@@ -45,8 +47,6 @@
     got_a,
     send_b,
     got_b,
-    mult,
-    prim,
     part_out,
     part_in,
     local_sem,
@@ -63,8 +63,13 @@
         return carry
 
     lax.fori_loop(1, PANELS, greet, 0)
-    load = pltpu.make_async_copy(rec_hbm.at[0], rec, local_sem.at[0])
-    load.start()
+    loads = [
+        pltpu.make_async_copy(receiver_hbm.at[0], raw.at[0], local_sem.at[0]),
+        pltpu.make_async_copy(source_hbm.at[0], raw.at[1], local_sem.at[1]),
+        pltpu.make_async_copy(rec_hbm.at[0], rec, local_sem.at[2]),
+    ]
+    for load in loads:
+        load.start()
 
     def build(index, carry):
         build_operator(taps_ref, oper, index)
@@ -100,8 +105,12 @@
             def _():
                 dst[me] = src[me]
 
+    loads[0].wait()
+    taps_ref[...] = jnp.zeros_like(taps_ref)
+    taps_ref[0:2, 0 : TAPS - 1] = raw[0].astype(jnp.float32)
+    taps_ref[0:2, :] = pltpu.roll(taps_ref[0:8, :], 1, 1)[0:2]
     lax.fori_loop(0, 2, build, 0)
-    load.wait()
+    loads[2].wait()
     data_re = rec[0].astype(jnp.bfloat16)
     data_im = rec[1].astype(jnp.bfloat16)
     left[0:ROWS, :] = data_re
@@ -137,6 +146,17 @@
         return carry
 
     lax.fori_loop(0, BLOCKS, forward, 0)
+    loads[1].wait()
+    taps_ref[8:10, 0 : TAPS - 1] = raw[1].astype(jnp.float32)
+    mirror = (
+        lax.broadcasted_iota(jnp.int32, (128, 128), 0)
+        + lax.broadcasted_iota(jnp.int32, (128, 128), 1)
+        == 127
+    ).astype(jnp.bfloat16)
+    for g in range(TAPS // 128):
+        piece = taps_ref[8:16, 128 * g : 128 * g + 128].astype(jnp.bfloat16)
+        turned = jnp.dot(piece, mirror, preferred_element_type=jnp.float32)
+        taps_ref[2:4, TAPS - 128 * (g + 1) : TAPS - 128 * g] = turned[0:2]
     lax.fori_loop(2, 4, build, 0)
 
     def wait_received(stage, src, dst, sender):
@@ -190,8 +210,8 @@
         re = jnp.where(low_half, even, pltpu.roll(odd, ROWS, 1))
         im = jnp.where(low_half, pltpu.roll(even, ROWS, 1), odd)
         at = pl.ds(pl.multiple_of(pair * 128, 128), 128)
-        mult[0, :, at] = re.astype(jnp.bfloat16)
-        mult[1, :, at] = im.astype(jnp.bfloat16)
+        mult[0, 0, :, at] = re.astype(jnp.bfloat16)
+        mult[0, 1, :, at] = im.astype(jnp.bfloat16)
         data_re = rec[0, :, at]
         data_im = rec[1, :, at]
         return (
@@ -205,8 +225,6 @@
     part_out[0:8] = num_re
     part_out[8:16] = num_im
     part_out[16:24] = energy
-    keep = pltpu.make_async_copy(mult, mult_hbm.at[0], local_sem.at[1])
-    keep.start()
 
     def share(k, wait):
         target = lax.rem(me + k, PANELS)
@@ -246,28 +264,22 @@
 
     def subtract(pair, carry):
         at = pl.ds(pl.multiple_of(pair * 128, 128), 128)
-        re = mult[0, :, at].astype(jnp.float32)
-        im = mult[1, :, at].astype(jnp.float32)
-        prim[0, :, at] = rec[0, :, at] - (fit_re * re - fit_im * im)
-        prim[1, :, at] = rec[1, :, at] - (fit_re * im + fit_im * re)
+        re = mult[0, 0, :, at].astype(jnp.float32)
+        im = mult[0, 1, :, at].astype(jnp.float32)
+        prim[0, 0, :, at] = rec[0, :, at] - (fit_re * re - fit_im * im)
+        prim[0, 1, :, at] = rec[1, :, at] - (fit_re * im + fit_im * re)
         return carry
 
     lax.fori_loop(0, PAIRS, subtract, 0)
-    store = pltpu.make_async_copy(prim, prim_hbm.at[0], local_sem.at[2])
-    store.start()
 
     def share_done(k, carry):
         share(k, True).wait_send()
         return carry
 
     lax.fori_loop(1, PANELS, share_done, 0)
-    keep.wait()
-    store.wait()
 
 
 def per_device(recorded, receiver_kernel, source_kernel):
-    taps = jnp.concatenate([receiver_kernel[0], jnp.flip(source_kernel[0], axis=1)], axis=0)
-    taps = jnp.pad(taps.astype(jnp.float32), ((0, 4), (0, 1)))
     vmem = pltpu.VMEM
     return pl.pallas_call(
         kernel,
@@ -276,15 +288,18 @@
             jax.ShapeDtypeStruct((1, 2, ROWS, WIDTH), jnp.bfloat16),
         ),
         in_specs=[
-            pl.BlockSpec(memory_space=pl.ANY),
-            pl.BlockSpec(memory_space=pltpu.VMEM),
+            pl.BlockSpec(memory_space=pltpu.HBM),
+            pl.BlockSpec(memory_space=pltpu.HBM),
+            pl.BlockSpec(memory_space=pltpu.HBM),
         ],
         out_specs=(
-            pl.BlockSpec(memory_space=pl.ANY),
-            pl.BlockSpec(memory_space=pl.ANY),
+            pl.BlockSpec(memory_space=pltpu.VMEM),
+            pl.BlockSpec(memory_space=pltpu.VMEM),
         ),
         scratch_shapes=[
             vmem((2, ROWS, WIDTH), jnp.float32),
+            vmem((2, 2, TAPS - 1), jnp.bfloat16),
+            vmem((16, TAPS), jnp.float32),
             vmem((4, 128 * UNITS, BLOCK), jnp.bfloat16),
             vmem((2 * ROWS, WIDTH), jnp.bfloat16),
             vmem((2 * ROWS, WIDTH), jnp.bfloat16),
@@ -292,8 +307,6 @@
             vmem((PANELS, ROWS, 128), jnp.bfloat16),
             vmem((PANELS, ROWS, 128), jnp.bfloat16),
             vmem((PANELS, ROWS, 128), jnp.bfloat16),
-            vmem((2, ROWS, WIDTH), jnp.bfloat16),
-            vmem((2, ROWS, WIDTH), jnp.float32),
             vmem((24, 128), jnp.float32),
             vmem((PANELS, 24, 128), jnp.float32),
             pltpu.SemaphoreType.DMA((3,)),
@@ -303,7 +316,7 @@
         compiler_params=pltpu.CompilerParams(
             collective_id=0, has_side_effects=True, vmem_limit_bytes=48 * 1024 * 1024
         ),
-    )(recorded, taps)
+    )(recorded, receiver_kernel, source_kernel)
 
 
 def solution(mesh):

time: 72.7 us -> 61.3 us (0.84)
  the two profiles are of different devices: /device:TPU:1 before, /device:TPU:25 now
where the time goes in v2:
time: 61.3 us; the launch traced here: 61 us
  Pallas kernels  55.9 us (91%)
  local copies, waits for them, and re-layouts  4.42 us (7%)
  between operations  0.65 us (1%)
    pallas_call x1, Pallas kernels, per_device(): pl.pallas_call(kernel, out_shape=(jax.ShapeDtypeStruct((1, 2, ROWS, WIDTH...  55.9 us
    unnamed x8, local copies, waits for them, and re-layouts  4.42 us

profile of v2, /device:TPU:25, one launch (start us, length us, event | category | flops | bytes accessed | tf_op | source)
XLA Modules:
  0.0 61.0 jit_solution(10323463945401872514)
XLA Ops:
  0.6 0.0 copy-start
  0.6 1.2 %copy-done = f32[1,2,64,2048]{3,2,1,0:T(8,128)S(1)} copy-done((f32[1,2,64,2048]{3,2,1,0:T(8,128)S(1)}, f32[1,2,64,2048]{3,2,1,0:T(8,128)}, u32[]{:S(2)}) %copy-start) | copy-done | bytes 1048600
  1.9 0.0 copy-start.1
  1.9 0.7 %copy-done.1 = bf16[1,2,4095]{2,1,0:T(2,128)(2,1)S(1)} copy-done((bf16[1,2,4095]{2,1,0:T(2,128)(2,1)S(1)}, bf16[1,2,4095]{2,1,0:T(2,128)(2,1)}, u32[]{:S(2)}) %copy-start.1) | copy-done | bytes 16404
  2.6 0.0 copy-start.2
  2.6 0.7 %copy-done.2 = bf16[1,2,4095]{2,1,0:T(2,128)(2,1)S(1)} copy-done((bf16[1,2,4095]{2,1,0:T(2,128)(2,1)S(1)}, bf16[1,2,4095]{2,1,0:T(2,128)(2,1)}, u32[]{:S(2)}) %copy-start.2) | copy-done | bytes 16404
  3.3 55.9 %shard_map.50 = (f32[1,2,64,2048]{3,2,1,0:T(8,128)S(1)}, bf16[1,2,64,2048]{3,2,1,0:T(8,128)(2,1)S(1)}) custom-call(f32[1,2,64,2048]{3,2,1,0:T(8,128)S(1)} %copy-done, bf16[1,2,4095]{2,1,0:T(2,128)(2,1)S(1)} %copy-done.1, bf16[1,2,4095]{2,1,0:T(2,128)(2,1)S(1)} %copy-done.2), custom_call_target="tpu_custom_call" | custom-call | tf_op jit(solution)/shard_map/pallas_call | solution.py:284
  59.2 1.0 %copy.7 = f32[1,2,64,2048]{3,2,1,0:T(8,128)} copy(f32[1,2,64,2048]{3,2,1,0:T(8,128)S(1)} %get-tuple-element.4) | data formatting | bytes 2097152
  60.2 0.8 %copy.8 = bf16[1,2,64,2048]{3,2,1,0:T(8,128)(2,1)} copy(bf16[1,2,64,2048]{3,2,1,0:T(8,128)(2,1)S(1)} %get-tuple-element.5) | data formatting | bytes 1048576
Async XLA Ops:
  0.6 1.2 %copy-start = (f32[1,2,64,2048]{3,2,1,0:T(8,128)S(1)}, f32[1,2,64,2048]{3,2,1,0:T(8,128)}, u32[]{:S(2)}) copy-start(f32[1,2,64,2048]{3,2,1,0:T(8,128)} %rec_hbm.1) | copy-start | bytes 3145732
  1.9 0.7 %copy-start.1 = (bf16[1,2,4095]{2,1,0:T(2,128)(2,1)S(1)}, bf16[1,2,4095]{2,1,0:T(2,128)(2,1)}, u32[]{:S(2)}) copy-start(bf16[1,2,4095]{2,1,0:T(2,128)(2,1)} %receiver_hbm.1) | copy-start | bytes 49144
  2.6 0.7 %copy-start.2 = (bf16[1,2,4095]{2,1,0:T(2,128)(2,1)S(1)}, bf16[1,2,4095]{2,1,0:T(2,128)(2,1)}, u32[]{:S(2)}) copy-start(bf16[1,2,4095]{2,1,0:T(2,128)(2,1)} %source_hbm.1) | copy-start | bytes 49144

commit v3 on v0

v3 whole, which is shorter than its diff:
```python
import jax
import jax.numpy as jnp
from jax import lax
from jax.experimental import pallas as pl
from jax.experimental.pallas import tpu as pltpu
from jax.sharding import PartitionSpec as P

MESH = pl.DeviceIdType.MESH
PANELS = 32
ROWS = 64
WIDTH = PANELS * ROWS
BLOCK = 256
BLOCKS = WIDTH // BLOCK
TAPS = 2 * WIDTH
UNITS = 2 * (2 * BLOCKS - 1)
CHUNKS = 2
SUB = ROWS // CHUNKS
HALF = WIDTH // 2
GROUP = 8
GROUPS = PANELS // GROUP


def rolled_taps(taps_ref, index, e):
    skew = pltpu.roll(
        jnp.broadcast_to(taps_ref[pl.ds(index, 1), :], (8, TAPS)), 0, 1, stride=1, stride_axis=0
    )
    low = pltpu.roll(skew, 16 * e + TAPS - 128, 1)
    high = pltpu.roll(skew, 16 * e + 8 + TAPS - 128, 1)
    return jnp.concatenate([low, high], axis=0).astype(jnp.bfloat16)


def spread(parts, quarter):
    outs = []
    for i in range(4):
        out = parts[i]
        for k in range(4):
            if k != i:
                out = jnp.where(quarter == k, pltpu.roll(parts[k], 32 * (k - i) % 128, 1), out)
        outs.append(out)
    return outs


def kernel(
    rec,
    receiver_taps,
    source_taps,
    prim,
    mult,
    taps_ref,
    oper,
    skewed,
    mixed,
    left,
    left_turned,
    half,
    half_turned,
    send_a,
    got_a,
    send_b,
    got_b,
    part_out,
    part_in,
    send_sem,
    recv_sem,
):
    me = lax.axis_index("panel")
    my_group, my_seat = me // GROUP, lax.rem(me, GROUP)
    barrier = pltpu.get_barrier_semaphore()

    def greet(k, carry):
        pl.semaphore_signal(
            barrier, inc=1, device_id={"panel": lax.rem(me + k, PANELS)}, device_id_type=MESH
        )
        return carry

    lax.fori_loop(1, PANELS, greet, 0)

    def exchange(stage, src, dst, chunk, target):
        return pltpu.make_async_remote_copy(
            src_ref=src.at[chunk, target],
            dst_ref=dst.at[chunk, me],
            send_sem=send_sem.at[stage, chunk],
            recv_sem=recv_sem.at[stage, chunk],
            device_id={"panel": target},
            device_id_type=MESH,
        )

    def whole(stage, src, dst, chunk):
        others = pl.ds(0, PANELS - 1)
        return pltpu.make_async_remote_copy(
            src_ref=src.at[chunk, others],
            dst_ref=dst.at[chunk, others],
            send_sem=send_sem.at[stage, chunk],
            recv_sem=recv_sem.at[stage, chunk],
            device_id={"panel": lax.rem(me + 1, PANELS)},
            device_id_type=MESH,
        )

    def post(stage, src, dst, chunk, target):
        @pl.when(target != me)
        def _():
            exchange(stage, src, dst, chunk, target).start()

        @pl.when(target == me)
        def _():
            dst[chunk, me] = src[chunk, me]

    taps_ref[...] = jnp.zeros_like(taps_ref)
    taps_ref[0:2, 0 : TAPS - 1] = receiver_taps[0].astype(jnp.float32)
    taps_ref[0:2, :] = pltpu.roll(taps_ref[0:8, :], 1, 1)[0:2]

    def build_receiver(index, carry):
        for e in range(8):
            rows = rolled_taps(taps_ref, index, e)
            for u in range(UNITS):
                at = 128 * (UNITS - 1 - u)
                oper[index, 128 * u + 16 * e : 128 * u + 16 * e + 16, :] = rows[:, at : at + 256]
        return carry

    lax.fori_loop(0, 2, build_receiver, 0)
    data_re = rec[0, 0].astype(jnp.bfloat16)
    data_im = rec[0, 1].astype(jnp.bfloat16)
    left[0:ROWS, :] = data_re
    left[ROWS : 2 * ROWS, :] = data_im
    left_turned[0:ROWS, :] = -data_im
    left_turned[ROWS : 2 * ROWS, :] = data_re
    quarter = lax.broadcasted_iota(jnp.int32, (SUB, 128), 1) // 32

    def forward(step, carry):
        chunk, turn = step // GROUPS, lax.rem(step, GROUPS)
        shift = (turn + 1) // 2
        away = jnp.where(lax.rem(turn, 2) == 0, GROUPS // 2 + shift, GROUPS // 2 - shift)
        group = lax.rem(my_group + away, GROUPS)
        at = pl.multiple_of((BLOCKS - 1 - chunk * GROUPS - group) * BLOCK, BLOCK)
        result = jnp.dot(
            left[...], oper[0, pl.ds(at, WIDTH), :], preferred_element_type=jnp.float32
        ) + jnp.dot(
            left_turned[...], oper[1, pl.ds(at, WIDTH), :], preferred_element_type=jnp.float32
        )
        for g in range(2):
            lanes = slice(128 * g, 128 * g + 128)
            parts = [
                result[ROWS * comp + SUB * h : ROWS * comp + SUB * h + SUB, lanes]
                for h in range(2)
                for comp in range(2)
            ]
            for i, out in enumerate(spread(parts, quarter)):
                send_a[chunk, group * GROUP + 4 * g + i] = out.astype(jnp.bfloat16)

        @pl.when(step == 0)
        def _():
            pl.semaphore_wait(barrier, PANELS - 1)

        def one(t, inner):
            post(0, send_a, got_a, chunk, group * GROUP + lax.rem(my_seat + t, GROUP))
            return inner

        lax.fori_loop(0, GROUP, one, 0)
        return carry

    lax.fori_loop(0, BLOCKS, forward, 0)

    taps_ref[8:10, 0 : TAPS - 1] = source_taps[0].astype(jnp.float32)
    mirror = (
        lax.broadcasted_iota(jnp.int32, (128, 128), 0)
        + lax.broadcasted_iota(jnp.int32, (128, 128), 1)
        == 127
    ).astype(jnp.bfloat16)
    for g in range(TAPS // 128):
        piece = taps_ref[8:16, 128 * g : 128 * g + 128].astype(jnp.bfloat16)
        turned = jnp.dot(piece, mirror, preferred_element_type=jnp.float32)
        taps_ref[2:4, TAPS - 128 * (g + 1) : TAPS - 128 * g] = turned[0:2]
    narrow = lax.broadcasted_iota(jnp.int32, (16, 128), 1) // 32

    def build_source(comp, carry):
        for e in range(8):
            skewed[16 * e : 16 * e + 16, :] = rolled_taps(taps_ref, 2 + comp, e)

        def unit(u, inner):
            for e in range(8):
                to = pl.ds(pl.multiple_of(64 * u + 32 * (e // 4) + 16 * (e % 2), 16), 16)
                for h in range(2):
                    out = None
                    for i in range(4):
                        back = 2 * (i + h)
                        tile = UNITS - 1 - u + (1 if e < back else 0)
                        row = 16 * ((e - back) % 8)
                        piece = skewed[row : row + 16, pl.ds(pl.multiple_of(tile * 128, 128), 128)]
                        piece = piece.astype(jnp.float32)
                        out = piece if out is None else jnp.where(narrow == i, piece, out)
                    mixed[comp, (e // 2) % 2, to, 128 * h : 128 * h + 128] = out.astype(jnp.bfloat16)
            return inner

        lax.fori_loop(0, UNITS, unit, 0)
        return carry

    lax.fori_loop(0, 2, build_source, 0)
    first_block = me // 4

    def second(chunk, carry):
        whole(0, send_a, got_a, chunk).wait_recv()

        def turn(g, inner):
            block = jnp.concatenate([got_a[chunk, 4 * g + i] for i in range(4)], axis=0)
            flipped = block.astype(jnp.float32).T
            at = pl.ds(pl.multiple_of(g * 128, 128), 128)
            for h in range(2):
                re = flipped[2 * SUB * h : 2 * SUB * h + SUB]
                im = flipped[2 * SUB * h + SUB : 2 * SUB * (h + 1)]
                half[h, 0:SUB, at] = re.astype(jnp.bfloat16)
                half[h, SUB : 2 * SUB, at] = im.astype(jnp.bfloat16)
                half_turned[h, 0:SUB, at] = (-im).astype(jnp.bfloat16)
                half_turned[h, SUB : 2 * SUB, at] = re.astype(jnp.bfloat16)
            return inner

        lax.fori_loop(0, PANELS // 4, turn, 0)

        def backward(step, inner):
            shift = (step + 1) // 2
            away = jnp.where(lax.rem(step, 2) == 0, BLOCKS // 2 + shift, BLOCKS // 2 - shift)
            block = lax.rem(first_block + away, BLOCKS)
            at = pl.ds(pl.multiple_of((BLOCKS - 1 - block) * 128, 128), HALF)
            result = None
            for h in range(2):
                for comp, lhs in enumerate((half, half_turned)):
                    term = jnp.dot(lhs[h], mixed[comp, h, at, :], preferred_element_type=jnp.float32)
                    result = term if result is None else result + term
            stacked = jnp.concatenate([result[:, 0:128], result[:, 128:256]], axis=0)
            rows = stacked.T.astype(jnp.bfloat16)
            for i in range(4):
                send_b[chunk, block * 4 + i] = rows[SUB * i : SUB * i + SUB]
                post(1, send_b, got_b, chunk, block * 4 + i)
            return inner

        lax.fori_loop(0, BLOCKS, backward, 0)
        return carry

    lax.fori_loop(0, CHUNKS, second, 0)

    def fold(x):
        total = x[0:8]
        for k in range(1, SUB // 8):
            total = total + x[8 * k : 8 * k + 8]
        return total

    def collect(chunk, sums):
        whole(1, send_b, got_b, chunk).wait_recv()

        def tile(g, sums):
            parts = [got_b[chunk, 4 * g + i].astype(jnp.float32) for i in range(4)]
            outs = spread(parts, quarter)
            at = pl.ds(pl.multiple_of(chunk * HALF + g * 128, 128), 128)
            num_re, num_im, energy = sums
            for h in range(2):
                re, im = outs[2 * h], outs[2 * h + 1]
                rows = slice(SUB * h, SUB * h + SUB)
                mult[0, 0, rows, at] = re.astype(jnp.bfloat16)
                mult[0, 1, rows, at] = im.astype(jnp.bfloat16)
                data_re = rec[0, 0, rows, at]
                data_im = rec[0, 1, rows, at]
                num_re = num_re + fold(re * data_re + im * data_im)
                num_im = num_im + fold(re * data_im - im * data_re)
                energy = energy + fold(re * re + im * im)
            return num_re, num_im, energy

        return lax.fori_loop(0, PANELS // 4, tile, sums)

    zero = jnp.zeros((8, 128), jnp.float32)
    sums = lax.fori_loop(0, CHUNKS, collect, (zero, zero, zero))
    column = lax.broadcasted_iota(jnp.int32, (1, 128), 1)
    sums = [jnp.sum(x, keepdims=True) for x in sums]
    mine = jnp.where(column == 0, sums[0], jnp.where(column == 1, sums[1], sums[2]))
    part_out[0:1, 0:1] = mine[None]
    part_in[pl.ds(me, 1), 0:1] = mine[None]

    def share(k, carry):
        target = lax.rem(me + k, PANELS)
        pltpu.make_async_remote_copy(
            src_ref=part_out.at[pl.ds(0, 1), pl.ds(0, 1)],
            dst_ref=part_in.at[pl.ds(me, 1), pl.ds(0, 1)],
            send_sem=send_sem.at[2, 0],
            recv_sem=recv_sem.at[2, 0],
            device_id={"panel": target},
            device_id_type=MESH,
        ).start()
        return carry

    lax.fori_loop(1, PANELS, share, 0)
    for chunk in range(CHUNKS):
        whole(0, send_a, got_a, chunk).wait_send()
        whole(1, send_b, got_b, chunk).wait_send()
    others = pl.ds(0, PANELS - 1)
    shared = pltpu.make_async_remote_copy(
        src_ref=part_in.at[others, pl.ds(0, 1)],
        dst_ref=part_in.at[others, pl.ds(0, 1)],
        send_sem=send_sem.at[2, 0],
        recv_sem=recv_sem.at[2, 0],
        device_id={"panel": lax.rem(me + 1, PANELS)},
        device_id_type=MESH,
    )
    shared.wait_recv()
    total = part_in[0, 0:1]
    for k in range(1, PANELS):
        total = total + part_in[k, 0:1]
    den = total[:, 2:3] + 1e-06
    fit_re = total[:, 0:1] / den
    fit_im = total[:, 1:2] / den

    def subtract(pair, carry):
        at = pl.ds(pl.multiple_of(pair * 128, 128), 128)
        re = mult[0, 0, :, at].astype(jnp.float32)
        im = mult[0, 1, :, at].astype(jnp.float32)
        prim[0, 0, :, at] = rec[0, 0, :, at] - (fit_re * re - fit_im * im)
        prim[0, 1, :, at] = rec[0, 1, :, at] - (fit_re * im + fit_im * re)
        return carry

    lax.fori_loop(0, WIDTH // 128, subtract, 0)
    shared.wait_send()


def per_device(recorded, receiver_kernel, source_kernel):
    vmem = pltpu.VMEM
    bf16 = jnp.bfloat16
    return pl.pallas_call(
        kernel,
        out_shape=(
            jax.ShapeDtypeStruct((1, 2, ROWS, WIDTH), jnp.float32),
            jax.ShapeDtypeStruct((1, 2, ROWS, WIDTH), bf16),
        ),
        in_specs=[pl.BlockSpec(memory_space=vmem)] * 3,
        out_specs=(pl.BlockSpec(memory_space=vmem), pl.BlockSpec(memory_space=vmem)),
        scratch_shapes=[
            vmem((16, TAPS), jnp.float32),
            vmem((2, 128 * UNITS, BLOCK), bf16),
            vmem((128, TAPS), bf16),
            vmem((2, 2, 64 * UNITS, BLOCK), bf16),
            vmem((2 * ROWS, WIDTH), bf16),
            vmem((2 * ROWS, WIDTH), bf16),
            vmem((2, 2 * SUB, HALF), bf16),
            vmem((2, 2 * SUB, HALF), bf16),
            vmem((CHUNKS, PANELS, SUB, 128), bf16),
            vmem((CHUNKS, PANELS, SUB, 128), bf16),
            vmem((CHUNKS, PANELS, SUB, 128), bf16),
            vmem((CHUNKS, PANELS, SUB, 128), bf16),
            vmem((1, 8, 128), jnp.float32),
            vmem((PANELS, 8, 128), jnp.float32),
            pltpu.SemaphoreType.DMA((3, CHUNKS)),
            pltpu.SemaphoreType.DMA((3, CHUNKS)),
        ],
        compiler_params=pltpu.CompilerParams(
            collective_id=0, has_side_effects=True, vmem_limit_bytes=48 * 1024 * 1024
        ),
    )(recorded, receiver_kernel, source_kernel)


def solution(mesh):
    placed = (P("freq", None, "panel", None), P("freq", None, None), P("freq", None, None))
    return jax.shard_map(
        per_device,
        mesh=mesh,
        in_specs=placed,
        out_specs=(P("freq", None, "panel", None), P("freq", None, "panel", None)),
        check_vma=False,
    )
```

time: 459 us -> 54.8 us (0.12); the launches traced: 451 us -> 54.6 us
  local copies, waits for them, and re-layouts: 259 us -> 4.42 us
  waiting for transfers between devices: 106 us -> 0 us
  Pallas kernels: 0 us -> 49.5 us
  matrix products: 33.7 us -> 0 us
  blocking collectives: 29.6 us -> 0 us
  between operations: 16.3 us -> 0.65 us
  other arithmetic: 6.01 us -> 0 us
    unnamed x8, local copies, waits for them, and re-layouts: 122 us -> 4.42 us
    all_gather x1 -> x0, waiting for transfers between devices: 106 us -> none  [per_device(): lax.all_gather(focused, 'panel', axis=2, tiled=True)[0]]
    reshape x2 -> x0, local copies, waits for them, and re-layouts: 54.6 us -> none  [band(): return flat.reshape(2, nrows, length - 1)[:, :, :ncols]]
    another operation x4 -> x0, local copies, waits for them, and re-layouts: 52 us -> none  [band(): flat = jnp.tile(rolled, (1, nrows))[:, :nrows * (length - 1)]]
    pallas_call x0 -> x1, Pallas kernels: none -> 49.5 us  [per_device(): pl.pallas_call(kernel, out_shape=(jax.ShapeDtypeStruct((1, 2, ROWS, WIDTH...]
    dot_general x8 -> x0, matrix products: 33.7 us -> none  [the longest x2 10.6 us: complex_dot(): jnp.dot(left[1], right[0], preferred_element_type=jnp.float32)]
    slice x7 -> x0, local copies, waits for them, and re-layouts: 29.9 us -> none  [the longest x2 27.7 us: band(): flat = jnp.tile(rolled, (1, nrows))[:, :nrows * (length - 1)]]
    all_to_all x1 -> x0, blocking collectives: 29.6 us -> none  [from_everyone(): return lax.all_to_all(copies, axis, split_axis=0, concat_axis=0, tiled=True)]
  transfers between devices with their start and end apart: 1 -> 0, of which waited for: 1 -> 0; matrix products, arithmetic and copies ran while one was open for 1% -> 0% of each run, Pallas kernels for 0% -> 0%
where the time goes in v3:
time: 54.8 us; the launch traced here: 54.6 us
  Pallas kernels  49.5 us (90%)
  local copies, waits for them, and re-layouts  4.42 us (8%)
  between operations  0.65 us (1%)
    pallas_call x1, Pallas kernels, per_device(): pl.pallas_call(kernel, out_shape=(jax.ShapeDtypeStruct((1, 2, ROWS, WIDTH...  49.5 us
    unnamed x8, local copies, waits for them, and re-layouts  4.42 us

profile of v3, /device:TPU:1, one launch (start us, length us, event | category | flops | bytes accessed | tf_op | source)
XLA Modules:
  0.0 54.6 jit_solution(11772452474374716688)
XLA Ops:
  0.6 0.0 copy-start
  0.6 1.2 %copy-done = f32[1,2,64,2048]{3,2,1,0:T(8,128)S(1)} copy-done((f32[1,2,64,2048]{3,2,1,0:T(8,128)S(1)}, f32[1,2,64,2048]{3,2,1,0:T(8,128)}, u32[]{:S(2)}) %copy-start) | copy-done | bytes 1048600
  1.9 0.0 copy-start.1
  1.9 0.7 %copy-done.1 = bf16[1,2,4095]{2,1,0:T(2,128)(2,1)S(1)} copy-done((bf16[1,2,4095]{2,1,0:T(2,128)(2,1)S(1)}, bf16[1,2,4095]{2,1,0:T(2,128)(2,1)}, u32[]{:S(2)}) %copy-start.1) | copy-done | bytes 16404
  2.6 0.0 copy-start.2
  2.6 0.7 %copy-done.2 = bf16[1,2,4095]{2,1,0:T(2,128)(2,1)S(1)} copy-done((bf16[1,2,4095]{2,1,0:T(2,128)(2,1)S(1)}, bf16[1,2,4095]{2,1,0:T(2,128)(2,1)}, u32[]{:S(2)}) %copy-start.2) | copy-done | bytes 16404
  3.3 49.5 %shard_map.50 = (f32[1,2,64,2048]{3,2,1,0:T(8,128)S(1)}, bf16[1,2,64,2048]{3,2,1,0:T(8,128)(2,1)S(1)}) custom-call(f32[1,2,64,2048]{3,2,1,0:T(8,128)S(1)} %copy-done, bf16[1,2,4095]{2,1,0:T(2,128)(2,1)S(1)} %copy-done.1, bf16[1,2,4095]{2,1,0:T(2,128)(2,1)S(1)} %copy-done.2), custom_call_target="tpu_custom_call" | custom-call | tf_op jit(solution)/shard_map/pallas_call | solution.py:324
  52.8 1.0 %copy.7 = f32[1,2,64,2048]{3,2,1,0:T(8,128)} copy(f32[1,2,64,2048]{3,2,1,0:T(8,128)S(1)} %get-tuple-element.4) | data formatting | bytes 2097152
  53.8 0.8 %copy.8 = bf16[1,2,64,2048]{3,2,1,0:T(8,128)(2,1)} copy(bf16[1,2,64,2048]{3,2,1,0:T(8,128)(2,1)S(1)} %get-tuple-element.5) | data formatting | bytes 1048576
Async XLA Ops:
  0.6 1.2 %copy-start = (f32[1,2,64,2048]{3,2,1,0:T(8,128)S(1)}, f32[1,2,64,2048]{3,2,1,0:T(8,128)}, u32[]{:S(2)}) copy-start(f32[1,2,64,2048]{3,2,1,0:T(8,128)} %rec.1) | copy-start | bytes 3145732
  1.9 0.7 %copy-start.1 = (bf16[1,2,4095]{2,1,0:T(2,128)(2,1)S(1)}, bf16[1,2,4095]{2,1,0:T(2,128)(2,1)}, u32[]{:S(2)}) copy-start(bf16[1,2,4095]{2,1,0:T(2,128)(2,1)} %receiver_taps.1) | copy-start | bytes 49144
  2.6 0.7 %copy-start.2 = (bf16[1,2,4095]{2,1,0:T(2,128)(2,1)S(1)}, bf16[1,2,4095]{2,1,0:T(2,128)(2,1)}, u32[]{:S(2)}) copy-start(bf16[1,2,4095]{2,1,0:T(2,128)(2,1)} %source_taps.1) | copy-start | bytes 49144

commit v4 on v3

--- a/solution.py
+++ b/solution.py
@@ -41,11 +41,13 @@
 
 
 def kernel(
-    rec,
-    receiver_taps,
-    source_taps,
+    rec_hbm,
+    receiver_hbm,
+    source_hbm,
     prim,
     mult,
+    rec,
+    raw,
     taps_ref,
     oper,
     skewed,
@@ -60,6 +62,7 @@
     got_b,
     part_out,
     part_in,
+    load_sem,
     send_sem,
     recv_sem,
 ):
@@ -73,6 +76,13 @@
         )
         return carry
 
+    loads = [
+        pltpu.make_async_copy(receiver_hbm, raw.at[pl.ds(0, 1)], load_sem.at[0]),
+        pltpu.make_async_copy(rec_hbm, rec, load_sem.at[1]),
+        pltpu.make_async_copy(source_hbm, raw.at[pl.ds(1, 1)], load_sem.at[2]),
+    ]
+    for load in loads:
+        load.start()
     lax.fori_loop(1, PANELS, greet, 0)
 
     def exchange(stage, src, dst, chunk, target):
@@ -106,7 +116,8 @@
             dst[chunk, me] = src[chunk, me]
 
     taps_ref[...] = jnp.zeros_like(taps_ref)
-    taps_ref[0:2, 0 : TAPS - 1] = receiver_taps[0].astype(jnp.float32)
+    loads[0].wait()
+    taps_ref[0:2, 0 : TAPS - 1] = raw[0].astype(jnp.float32)
     taps_ref[0:2, :] = pltpu.roll(taps_ref[0:8, :], 1, 1)[0:2]
 
     def build_receiver(index, carry):
@@ -118,6 +129,7 @@
         return carry
 
     lax.fori_loop(0, 2, build_receiver, 0)
+    loads[1].wait()
     data_re = rec[0, 0].astype(jnp.bfloat16)
     data_im = rec[0, 1].astype(jnp.bfloat16)
     left[0:ROWS, :] = data_re
@@ -160,7 +172,8 @@
 
     lax.fori_loop(0, BLOCKS, forward, 0)
 
-    taps_ref[8:10, 0 : TAPS - 1] = source_taps[0].astype(jnp.float32)
+    loads[2].wait()
+    taps_ref[8:10, 0 : TAPS - 1] = raw[1].astype(jnp.float32)
     mirror = (
         lax.broadcasted_iota(jnp.int32, (128, 128), 0)
         + lax.broadcasted_iota(jnp.int32, (128, 128), 1)
@@ -178,7 +191,8 @@
 
         def unit(u, inner):
             for e in range(8):
-                to = pl.ds(pl.multiple_of(64 * u + 32 * (e // 4) + 16 * (e % 2), 16), 16)
+                at = 256 * (u // 2) + 128 * ((e // 2) % 2) + 64 * lax.rem(u, 2)
+                to = pl.ds(pl.multiple_of(at + 32 * (e // 4) + 16 * (e % 2), 16), 16)
                 for h in range(2):
                     out = None
                     for i in range(4):
@@ -188,51 +202,59 @@
                         piece = skewed[row : row + 16, pl.ds(pl.multiple_of(tile * 128, 128), 128)]
                         piece = piece.astype(jnp.float32)
                         out = piece if out is None else jnp.where(narrow == i, piece, out)
-                    mixed[comp, (e // 2) % 2, to, 128 * h : 128 * h + 128] = out.astype(jnp.bfloat16)
+                    mixed[comp, to, 128 * h : 128 * h + 128] = out.astype(jnp.bfloat16)
             return inner
 
         lax.fori_loop(0, UNITS, unit, 0)
         return carry
 
     lax.fori_loop(0, 2, build_source, 0)
-    first_block = me // 4
+    for buffer in (half, half_turned):
+        buffer[0 : 2 * SUB, 0:BLOCK] = jnp.zeros((2 * SUB, BLOCK), jnp.bfloat16)
+        buffer[2 * SUB : 4 * SUB, WIDTH : WIDTH + BLOCK] = jnp.zeros((2 * SUB, BLOCK), jnp.bfloat16)
 
     def second(chunk, carry):
         whole(0, send_a, got_a, chunk).wait_recv()
 
         def turn(g, inner):
             block = jnp.concatenate([got_a[chunk, 4 * g + i] for i in range(4)], axis=0)
-            flipped = block.astype(jnp.float32).T
-            at = pl.ds(pl.multiple_of(g * 128, 128), 128)
+            flipped = block.T
             for h in range(2):
                 re = flipped[2 * SUB * h : 2 * SUB * h + SUB]
                 im = flipped[2 * SUB * h + SUB : 2 * SUB * (h + 1)]
-                half[h, 0:SUB, at] = re.astype(jnp.bfloat16)
-                half[h, SUB : 2 * SUB, at] = im.astype(jnp.bfloat16)
-                half_turned[h, 0:SUB, at] = (-im).astype(jnp.bfloat16)
-                half_turned[h, SUB : 2 * SUB, at] = re.astype(jnp.bfloat16)
+                for top, place in ((0, BLOCK), (2 * SUB, 0)):
+                    at = pl.ds(pl.multiple_of(g * BLOCK + place + 128 * h, 128), 128)
+                    half[top : top + SUB, at] = re
+                    half[top + SUB : top + 2 * SUB, at] = im
+                    half_turned[top : top + SUB, at] = -im
+                    half_turned[top + SUB : top + 2 * SUB, at] = re
             return inner
 
         lax.fori_loop(0, PANELS // 4, turn, 0)
 
         def backward(step, inner):
             shift = (step + 1) // 2
-            away = jnp.where(lax.rem(step, 2) == 0, BLOCKS // 2 + shift, BLOCKS // 2 - shift)
-            block = lax.rem(first_block + away, BLOCKS)
-            at = pl.ds(pl.multiple_of((BLOCKS - 1 - block) * 128, 128), HALF)
-            result = None
-            for h in range(2):
-                for comp, lhs in enumerate((half, half_turned)):
-                    term = jnp.dot(lhs[h], mixed[comp, h, at, :], preferred_element_type=jnp.float32)
-                    result = term if result is None else result + term
-            stacked = jnp.concatenate([result[:, 0:128], result[:, 128:256]], axis=0)
-            rows = stacked.T.astype(jnp.bfloat16)
-            for i in range(4):
-                send_b[chunk, block * 4 + i] = rows[SUB * i : SUB * i + SUB]
-                post(1, send_b, got_b, chunk, block * 4 + i)
+            away = jnp.where(lax.rem(step, 2) == 0, GROUPS // 2 + shift, GROUPS // 2 - shift)
+            group = lax.rem(my_group + away, GROUPS)
+            at = pl.multiple_of((BLOCKS - 2 - 2 * group) * BLOCK, BLOCK)
+            at = pl.ds(at, WIDTH + BLOCK)
+            result = jnp.dot(
+                half[...], mixed[0, at, :], preferred_element_type=jnp.float32
+            ) + jnp.dot(half_turned[...], mixed[1, at, :], preferred_element_type=jnp.float32)
+            for b in range(2):
+                part = result[2 * SUB * b : 2 * SUB * (b + 1)].astype(jnp.bfloat16)
+                rows = jnp.concatenate([part[:, 0:128], part[:, 128:256]], axis=0).T
+                for i in range(4):
+                    send_b[chunk, group * GROUP + 4 * b + i] = rows[SUB * i : SUB * i + SUB]
+
+            def one(t, inner2):
+                post(1, send_b, got_b, chunk, group * GROUP + lax.rem(my_seat + t, GROUP))
+                return inner2
+
+            lax.fori_loop(0, GROUP, one, 0)
             return inner
 
-        lax.fori_loop(0, BLOCKS, backward, 0)
+        lax.fori_loop(0, GROUPS, backward, 0)
         return carry
 
     lax.fori_loop(0, CHUNKS, second, 0)
@@ -318,7 +340,7 @@
     shared.wait_send()
 
 
-def per_device(recorded, receiver_kernel, source_kernel):
+def per_device(*operands):
     vmem = pltpu.VMEM
     bf16 = jnp.bfloat16
     return pl.pallas_call(
@@ -327,30 +349,33 @@
             jax.ShapeDtypeStruct((1, 2, ROWS, WIDTH), jnp.float32),
             jax.ShapeDtypeStruct((1, 2, ROWS, WIDTH), bf16),
         ),
-        in_specs=[pl.BlockSpec(memory_space=vmem)] * 3,
+        in_specs=[pl.BlockSpec(memory_space=pltpu.HBM)] * 3,
         out_specs=(pl.BlockSpec(memory_space=vmem), pl.BlockSpec(memory_space=vmem)),
         scratch_shapes=[
+            vmem((1, 2, ROWS, WIDTH), jnp.float32),
+            vmem((2, 2, TAPS - 1), bf16),
             vmem((16, TAPS), jnp.float32),
             vmem((2, 128 * UNITS, BLOCK), bf16),
             vmem((128, TAPS), bf16),
-            vmem((2, 2, 64 * UNITS, BLOCK), bf16),
+            vmem((2, 128 * UNITS, BLOCK), bf16),
             vmem((2 * ROWS, WIDTH), bf16),
             vmem((2 * ROWS, WIDTH), bf16),
-            vmem((2, 2 * SUB, HALF), bf16),
-            vmem((2, 2 * SUB, HALF), bf16),
+            vmem((4 * SUB, WIDTH + BLOCK), bf16),
+            vmem((4 * SUB, WIDTH + BLOCK), bf16),
             vmem((CHUNKS, PANELS, SUB, 128), bf16),
             vmem((CHUNKS, PANELS, SUB, 128), bf16),
             vmem((CHUNKS, PANELS, SUB, 128), bf16),
             vmem((CHUNKS, PANELS, SUB, 128), bf16),
             vmem((1, 8, 128), jnp.float32),
             vmem((PANELS, 8, 128), jnp.float32),
+            pltpu.SemaphoreType.DMA((3,)),
             pltpu.SemaphoreType.DMA((3, CHUNKS)),
             pltpu.SemaphoreType.DMA((3, CHUNKS)),
         ],
         compiler_params=pltpu.CompilerParams(
             collective_id=0, has_side_effects=True, vmem_limit_bytes=48 * 1024 * 1024
         ),
-    )(recorded, receiver_kernel, source_kernel)
+    )(*(pltpu.with_memory_space_constraint(x, pltpu.HBM) for x in operands))
 
 
 def solution(mesh):

time: 54.8 us -> 51.4 us (0.938)
  local copies, waits for them, and re-layouts: 4.42 us -> 1.77 us
  Pallas kernels: 49.5 us -> 48.8 us
    unnamed x8 -> x2, local copies, waits for them, and re-layouts: 4.42 us -> 1.77 us
    pallas_call x1, Pallas kernels: 49.5 us -> 48.8 us  [per_device(): pl.pallas_call(kernel, out_shape=(jax.ShapeDtypeStruct((1, 2, ROWS, WIDTH...]
where the time goes in v4:
time: 51.4 us; the launch traced here: 51.2 us
  Pallas kernels  48.8 us (95%)
  local copies, waits for them, and re-layouts  1.77 us (3%)
  between operations  0.64 us (1%)
    pallas_call x1, Pallas kernels, per_device(): pl.pallas_call(kernel, out_shape=(jax.ShapeDtypeStruct((1, 2, ROWS, WIDTH...  48.8 us
    unnamed x2, local copies, waits for them, and re-layouts  1.77 us

profile of v4, /device:TPU:1, one launch (start us, length us, event | category | flops | bytes accessed | tf_op | source)
XLA Modules:
  0.0 51.2 jit_solution(10452061859236988011)
XLA Ops:
  0.6 48.8 %shard_map.50 = (f32[1,2,64,2048]{3,2,1,0:T(8,128)S(1)}, bf16[1,2,64,2048]{3,2,1,0:T(8,128)(2,1)S(1)}) custom-call(f32[1,2,64,2048]{3,2,1,0:T(8,128)} %rec_hbm.1, bf16[1,2,4095]{2,1,0:T(2,128)(2,1)} %receiver_hbm.1, bf16[1,2,4095]{2,1,0:T(2,128)(2,1)} %source_hbm.1), custom_call_target="tpu_custom_call" | custom-call | tf_op jit(solution)/shard_map/pallas_call | solution.py:346
  49.4 1.0 %copy.7 = f32[1,2,64,2048]{3,2,1,0:T(8,128)} copy(f32[1,2,64,2048]{3,2,1,0:T(8,128)S(1)} %get-tuple-element.4) | data formatting | bytes 2097152
  50.4 0.8 %copy.8 = bf16[1,2,64,2048]{3,2,1,0:T(8,128)(2,1)} copy(bf16[1,2,64,2048]{3,2,1,0:T(8,128)(2,1)S(1)} %get-tuple-element.5) | data formatting | bytes 1048576

commit v5 on v4

--- a/solution.py
+++ b/solution.py
@@ -44,9 +44,9 @@
     rec_hbm,
     receiver_hbm,
     source_hbm,
-    prim,
     mult,
     rec,
+    sums_ref,
     raw,
     taps_ref,
     oper,
@@ -81,8 +81,14 @@
         pltpu.make_async_copy(rec_hbm, rec, load_sem.at[1]),
         pltpu.make_async_copy(source_hbm, raw.at[pl.ds(1, 1)], load_sem.at[2]),
     ]
-    for load in loads:
-        load.start()
+    loads[0].start()
+    for comp in range(2):
+        for piece in range(ROWS // 8):
+            rows = pl.ds(8 * piece, 8)
+            pltpu.make_async_copy(
+                rec_hbm.at[0, comp, rows], rec.at[0, comp, rows], load_sem.at[1]
+            ).start()
+    loads[2].start()
     lax.fori_loop(1, PANELS, greet, 0)
 
     def exchange(stage, src, dst, chunk, target):
@@ -90,21 +96,38 @@
             src_ref=src.at[chunk, target],
             dst_ref=dst.at[chunk, me],
             send_sem=send_sem.at[stage, chunk],
-            recv_sem=recv_sem.at[stage, chunk],
+            recv_sem=recv_sem.at[stage, chunk, my_group],
             device_id={"panel": target},
             device_id_type=MESH,
         )
 
-    def whole(stage, src, dst, chunk):
-        others = pl.ds(0, PANELS - 1)
+    def bulk(stage, src, dst, chunk, group, at, count):
+        slots = pl.ds(at, count)
         return pltpu.make_async_remote_copy(
-            src_ref=src.at[chunk, others],
-            dst_ref=dst.at[chunk, others],
+            src_ref=src.at[chunk, slots],
+            dst_ref=dst.at[chunk, slots],
             send_sem=send_sem.at[stage, chunk],
-            recv_sem=recv_sem.at[stage, chunk],
+            recv_sem=recv_sem.at[stage, chunk, group],
             device_id={"panel": lax.rem(me + 1, PANELS)},
             device_id_type=MESH,
         )
+
+    def sent(stage, src, dst, chunk):
+        bulk(stage, src, dst, chunk, 0, 0, PANELS - 1).wait_send()
+
+    def arrived(stage, src, dst, chunk, group):
+        @pl.when(group != my_group)
+        def _():
+            bulk(stage, src, dst, chunk, group, group * GROUP, GROUP).wait_recv()
+
+        @pl.when(group == my_group)
+        def _():
+            bulk(stage, src, dst, chunk, group, group * GROUP, GROUP - 1).wait_recv()
+
+    def group_of(turn):
+        shift = (turn + 1) // 2
+        away = jnp.where(lax.rem(turn, 2) == 0, GROUPS // 2 + shift, GROUPS // 2 - shift)
+        return lax.rem(my_group + away, GROUPS)
 
     def post(stage, src, dst, chunk, target):
         @pl.when(target != me)
@@ -139,10 +162,8 @@
     quarter = lax.broadcasted_iota(jnp.int32, (SUB, 128), 1) // 32
 
     def forward(step, carry):
-        chunk, turn = step // GROUPS, lax.rem(step, GROUPS)
-        shift = (turn + 1) // 2
-        away = jnp.where(lax.rem(turn, 2) == 0, GROUPS // 2 + shift, GROUPS // 2 - shift)
-        group = lax.rem(my_group + away, GROUPS)
+        chunk = step // GROUPS
+        group = group_of(lax.rem(step, GROUPS))
         at = pl.multiple_of((BLOCKS - 1 - chunk * GROUPS - group) * BLOCK, BLOCK)
         result = jnp.dot(
             left[...], oper[0, pl.ds(at, WIDTH), :], preferred_element_type=jnp.float32
@@ -214,9 +235,14 @@
         buffer[2 * SUB : 4 * SUB, WIDTH : WIDTH + BLOCK] = jnp.zeros((2 * SUB, BLOCK), jnp.bfloat16)
 
     def second(chunk, carry):
-        whole(0, send_a, got_a, chunk).wait_recv()
-
-        def turn(g, inner):
+        def turn(step, inner):
+            group = group_of(step // 2)
+            g = 2 * group + lax.rem(step, 2)
+
+            @pl.when(lax.rem(step, 2) == 0)
+            def _():
+                arrived(0, send_a, got_a, chunk, group)
+
             block = jnp.concatenate([got_a[chunk, 4 * g + i] for i in range(4)], axis=0)
             flipped = block.T
             for h in range(2):
@@ -233,9 +259,7 @@
         lax.fori_loop(0, PANELS // 4, turn, 0)
 
         def backward(step, inner):
-            shift = (step + 1) // 2
-            away = jnp.where(lax.rem(step, 2) == 0, GROUPS // 2 + shift, GROUPS // 2 - shift)
-            group = lax.rem(my_group + away, GROUPS)
+            group = group_of(step)
             at = pl.multiple_of((BLOCKS - 2 - 2 * group) * BLOCK, BLOCK)
             at = pl.ds(at, WIDTH + BLOCK)
             result = jnp.dot(
@@ -266,9 +290,14 @@
         return total
 
     def collect(chunk, sums):
-        whole(1, send_b, got_b, chunk).wait_recv()
-
-        def tile(g, sums):
+        def tile(step, sums):
+            group = group_of(step // 2)
+            g = 2 * group + lax.rem(step, 2)
+
+            @pl.when(lax.rem(step, 2) == 0)
+            def _():
+                arrived(1, send_b, got_b, chunk, group)
+
             parts = [got_b[chunk, 4 * g + i].astype(jnp.float32) for i in range(4)]
             outs = spread(parts, quarter)
             at = pl.ds(pl.multiple_of(chunk * HALF + g * 128, 128), 128)
@@ -301,7 +330,7 @@
             src_ref=part_out.at[pl.ds(0, 1), pl.ds(0, 1)],
             dst_ref=part_in.at[pl.ds(me, 1), pl.ds(0, 1)],
             send_sem=send_sem.at[2, 0],
-            recv_sem=recv_sem.at[2, 0],
+            recv_sem=recv_sem.at[2, 0, 0],
             device_id={"panel": target},
             device_id_type=MESH,
         ).start()
@@ -309,14 +338,14 @@
 
     lax.fori_loop(1, PANELS, share, 0)
     for chunk in range(CHUNKS):
-        whole(0, send_a, got_a, chunk).wait_send()
-        whole(1, send_b, got_b, chunk).wait_send()
+        sent(0, send_a, got_a, chunk)
+        sent(1, send_b, got_b, chunk)
     others = pl.ds(0, PANELS - 1)
     shared = pltpu.make_async_remote_copy(
         src_ref=part_in.at[others, pl.ds(0, 1)],
         dst_ref=part_in.at[others, pl.ds(0, 1)],
         send_sem=send_sem.at[2, 0],
-        recv_sem=recv_sem.at[2, 0],
+        recv_sem=recv_sem.at[2, 0, 0],
         device_id={"panel": lax.rem(me + 1, PANELS)},
         device_id_type=MESH,
     )
@@ -324,35 +353,52 @@
     total = part_in[0, 0:1]
     for k in range(1, PANELS):
         total = total + part_in[k, 0:1]
+    sums_ref[0:1] = total
+    shared.wait_send()
+
+
+def finish(mult, rec, sums_ref, prim_hbm, mult_hbm, prim, store_sem):
+    for comp in range(2):
+        for piece in range(ROWS // 16):
+            rows = pl.ds(16 * piece, 16)
+            pltpu.make_async_copy(
+                mult.at[0, comp, rows], mult_hbm.at[0, comp, rows], store_sem.at[0]
+            ).start()
+    total = sums_ref[0:1]
     den = total[:, 2:3] + 1e-06
-    fit_re = total[:, 0:1] / den
-    fit_im = total[:, 1:2] / den
-
-    def subtract(pair, carry):
-        at = pl.ds(pl.multiple_of(pair * 128, 128), 128)
-        re = mult[0, 0, :, at].astype(jnp.float32)
-        im = mult[0, 1, :, at].astype(jnp.float32)
-        prim[0, 0, :, at] = rec[0, 0, :, at] - (fit_re * re - fit_im * im)
-        prim[0, 1, :, at] = rec[0, 1, :, at] - (fit_re * im + fit_im * re)
-        return carry
-
-    lax.fori_loop(0, WIDTH // 128, subtract, 0)
-    shared.wait_send()
+    fit_re = jnp.broadcast_to(total[:, 0:1] / den, (16, 256))
+    fit_im = jnp.broadcast_to(total[:, 1:2] / den, (16, 256))
+    for piece in range(ROWS // 16):
+        rows = slice(16 * piece, 16 * piece + 16)
+        for pair in range(WIDTH // 256):
+            at = slice(256 * pair, 256 * pair + 256)
+            re = mult[0, 0, rows, at].astype(jnp.float32)
+            im = mult[0, 1, rows, at].astype(jnp.float32)
+            prim[0, 0, rows, at] = rec[0, 0, rows, at] - (fit_re * re - fit_im * im)
+            prim[0, 1, rows, at] = rec[0, 1, rows, at] - (fit_re * im + fit_im * re)
+        for comp in range(2):
+            for part in range(2):
+                eight = pl.ds(16 * piece + 8 * part, 8)
+                pltpu.make_async_copy(
+                    prim.at[0, comp, eight], prim_hbm.at[0, comp, eight], store_sem.at[1]
+                ).start()
+    pltpu.make_async_copy(mult, mult_hbm, store_sem.at[0]).wait()
+    pltpu.make_async_copy(prim, prim_hbm, store_sem.at[1]).wait()
 
 
 def per_device(*operands):
     vmem = pltpu.VMEM
     bf16 = jnp.bfloat16
-    return pl.pallas_call(
+    outs = (
+        jax.ShapeDtypeStruct((1, 2, ROWS, WIDTH), jnp.float32),
+        jax.ShapeDtypeStruct((1, 2, ROWS, WIDTH), bf16),
+    )
+    held = pl.pallas_call(
         kernel,
-        out_shape=(
-            jax.ShapeDtypeStruct((1, 2, ROWS, WIDTH), jnp.float32),
-            jax.ShapeDtypeStruct((1, 2, ROWS, WIDTH), bf16),
-        ),
+        out_shape=(outs[1], outs[0], jax.ShapeDtypeStruct((8, 128), jnp.float32)),
         in_specs=[pl.BlockSpec(memory_space=pltpu.HBM)] * 3,
-        out_specs=(pl.BlockSpec(memory_space=vmem), pl.BlockSpec(memory_space=vmem)),
+        out_specs=(pl.BlockSpec(memory_space=vmem),) * 3,
         scratch_shapes=[
-            vmem((1, 2, ROWS, WIDTH), jnp.float32),
             vmem((2, 2, TAPS - 1), bf16),
             vmem((16, TAPS), jnp.float32),
             vmem((2, 128 * UNITS, BLOCK), bf16),
@@ -370,12 +416,23 @@
             vmem((PANELS, 8, 128), jnp.float32),
             pltpu.SemaphoreType.DMA((3,)),
             pltpu.SemaphoreType.DMA((3, CHUNKS)),
-            pltpu.SemaphoreType.DMA((3, CHUNKS)),
+            pltpu.SemaphoreType.DMA((3, CHUNKS, GROUPS)),
         ],
         compiler_params=pltpu.CompilerParams(
             collective_id=0, has_side_effects=True, vmem_limit_bytes=48 * 1024 * 1024
         ),
     )(*(pltpu.with_memory_space_constraint(x, pltpu.HBM) for x in operands))
+    return pl.pallas_call(
+        finish,
+        out_shape=outs,
+        in_specs=[pl.BlockSpec(memory_space=vmem)] * 3,
+        out_specs=(pl.BlockSpec(memory_space=pltpu.HBM),) * 2,
+        scratch_shapes=[
+            vmem((1, 2, ROWS, WIDTH), jnp.float32),
+            pltpu.SemaphoreType.DMA((2,)),
+        ],
+        compiler_params=pltpu.CompilerParams(vmem_limit_bytes=16 * 1024 * 1024),
+    )(*held)
 
 
 def solution(mesh):

time: 51.4 us -> 48.8 us (0.949)
  local copies, waits for them, and re-layouts: 1.77 us -> 0 us
  Pallas kernels: 48.8 us -> 48 us
    unnamed x2 -> x0, local copies, waits for them, and re-layouts: 1.77 us -> none
    pallas_call x1 -> x2, Pallas kernels: 48.8 us -> 48 us  [the longest x1 46.8 us: per_device(): pl.pallas_call(kernel, out_shape=(outs[1], outs[0], jax.ShapeDtypeStruct(...]
where the time goes in v5:
time: 48.8 us; the launch traced here: 48.6 us
  Pallas kernels  48 us (98%)
  between operations  0.64 us (1%)
    pallas_call x1, Pallas kernels, per_device(): pl.pallas_call(kernel, out_shape=(outs[1], outs[0], jax.ShapeDtypeStruct(...  46.8 us
    pallas_call x1, Pallas kernels, per_device(): pl.pallas_call(finish, out_shape=outs, in_specs=[pl.BlockSpec(memory_spac...  1.19 us

profile of v5, /device:TPU:1, one launch (start us, length us, event | category | flops | bytes accessed | tf_op | source)
XLA Modules:
  0.0 48.6 jit_solution(3874543558805056255)
XLA Ops:
  0.6 46.8 %shard_map.50 = (bf16[1,2,64,2048]{3,2,1,0:T(8,128)(2,1)S(1)}, f32[1,2,64,2048]{3,2,1,0:T(8,128)S(1)}, f32[8,128]{1,0:T(8,128)S(1)}) custom-call(f32[1,2,64,2048]{3,2,1,0:T(8,128)} %rec_hbm.1, bf16[1,2,4095]{2,1,0:T(2,128)(2,1)} %receiver_hbm.1, bf16[1,2,4095]{2,1,0:T(2,128)(2,1)} %source_hbm.1), custom_call_target="tpu_custom_call" | custom-call | tf_op jit(solution)/shard_map/pallas_call | solution.py:396
  47.4 1.2 %shard_map.51 = (f32[1,2,64,2048]{3,2,1,0:T(8,128)}, bf16[1,2,64,2048]{3,2,1,0:T(8,128)(2,1)}) custom-call(bf16[1,2,64,2048]{3,2,1,0:T(8,128)(2,1)S(1)} %get-tuple-element.5.mult, f32[1,2,64,2048]{3,2,1,0:T(8,128)S(1)} %get-tuple-element.6.rec, f32[8,128]{1,0:T(8,128)S(1)} %get-tuple-element.7.sums_ref), custom_call_target="tpu_custom_call" | custom-call | tf_op jit(solution)/shard_map/pallas_call | solution.py:425

commit v6 on v5

--- a/solution.py
+++ b/solution.py
@@ -70,12 +70,6 @@
     my_group, my_seat = me // GROUP, lax.rem(me, GROUP)
     barrier = pltpu.get_barrier_semaphore()
 
-    def greet(k, carry):
-        pl.semaphore_signal(
-            barrier, inc=1, device_id={"panel": lax.rem(me + k, PANELS)}, device_id_type=MESH
-        )
-        return carry
-
     loads = [
         pltpu.make_async_copy(receiver_hbm, raw.at[pl.ds(0, 1)], load_sem.at[0]),
         pltpu.make_async_copy(rec_hbm, rec, load_sem.at[1]),
@@ -89,7 +83,10 @@
                 rec_hbm.at[0, comp, rows], rec.at[0, comp, rows], load_sem.at[1]
             ).start()
     loads[2].start()
-    lax.fori_loop(1, PANELS, greet, 0)
+    for k in range(1, PANELS):
+        pl.semaphore_signal(
+            barrier, inc=1, device_id={"panel": lax.rem(me + k, PANELS)}, device_id_type=MESH
+        )
 
     def exchange(stage, src, dst, chunk, target):
         return pltpu.make_async_remote_copy(
@@ -125,16 +122,18 @@
             bulk(stage, src, dst, chunk, group, group * GROUP, GROUP - 1).wait_recv()
 
     def group_of(turn):
-        shift = (turn + 1) // 2
-        away = jnp.where(lax.rem(turn, 2) == 0, GROUPS // 2 + shift, GROUPS // 2 - shift)
+        away = jnp.where(turn < 2, 2 * turn + 1, 6 - 2 * turn)
         return lax.rem(my_group + away, GROUPS)
 
-    def post(stage, src, dst, chunk, target):
-        @pl.when(target != me)
+    def post(stage, src, dst, chunk, group):
+        @pl.when(group != my_group)
         def _():
-            exchange(stage, src, dst, chunk, target).start()
-
-        @pl.when(target == me)
+            exchange(stage, src, dst, chunk, group * GROUP + my_seat).start()
+
+        for t in range(1, GROUP):
+            exchange(stage, src, dst, chunk, group * GROUP + lax.rem(my_seat + t, GROUP)).start()
+
+        @pl.when(group == my_group)
         def _():
             dst[chunk, me] = src[chunk, me]
 
@@ -184,11 +183,7 @@
         def _():
             pl.semaphore_wait(barrier, PANELS - 1)
 
-        def one(t, inner):
-            post(0, send_a, got_a, chunk, group * GROUP + lax.rem(my_seat + t, GROUP))
-            return inner
-
-        lax.fori_loop(0, GROUP, one, 0)
+        post(0, send_a, got_a, chunk, group)
         return carry
 
     lax.fori_loop(0, BLOCKS, forward, 0)
@@ -236,27 +231,24 @@
 
     def second(chunk, carry):
         def turn(step, inner):
-            group = group_of(step // 2)
-            g = 2 * group + lax.rem(step, 2)
-
-            @pl.when(lax.rem(step, 2) == 0)
-            def _():
-                arrived(0, send_a, got_a, chunk, group)
-
-            block = jnp.concatenate([got_a[chunk, 4 * g + i] for i in range(4)], axis=0)
-            flipped = block.T
-            for h in range(2):
-                re = flipped[2 * SUB * h : 2 * SUB * h + SUB]
-                im = flipped[2 * SUB * h + SUB : 2 * SUB * (h + 1)]
-                for top, place in ((0, BLOCK), (2 * SUB, 0)):
-                    at = pl.ds(pl.multiple_of(g * BLOCK + place + 128 * h, 128), 128)
-                    half[top : top + SUB, at] = re
-                    half[top + SUB : top + 2 * SUB, at] = im
-                    half_turned[top : top + SUB, at] = -im
-                    half_turned[top + SUB : top + 2 * SUB, at] = re
+            group = group_of(step)
+            arrived(0, send_a, got_a, chunk, group)
+            for part in range(2):
+                g = 2 * group + part
+                block = jnp.concatenate([got_a[chunk, 4 * g + i] for i in range(4)], axis=0)
+                flipped = block.T
+                for h in range(2):
+                    re = flipped[2 * SUB * h : 2 * SUB * h + SUB]
+                    im = flipped[2 * SUB * h + SUB : 2 * SUB * (h + 1)]
+                    for top, place in ((0, BLOCK), (2 * SUB, 0)):
+                        at = pl.ds(pl.multiple_of(g * BLOCK + place + 128 * h, 128), 128)
+                        half[top : top + SUB, at] = re
+                        half[top + SUB : top + 2 * SUB, at] = im
+                        half_turned[top : top + SUB, at] = -im
+                        half_turned[top + SUB : top + 2 * SUB, at] = re
             return inner
 
-        lax.fori_loop(0, PANELS // 4, turn, 0)
+        lax.fori_loop(0, GROUPS, turn, 0)
 
         def backward(step, inner):
             group = group_of(step)
@@ -270,12 +262,7 @@
                 rows = jnp.concatenate([part[:, 0:128], part[:, 128:256]], axis=0).T
                 for i in range(4):
                     send_b[chunk, group * GROUP + 4 * b + i] = rows[SUB * i : SUB * i + SUB]
-
-            def one(t, inner2):
-                post(1, send_b, got_b, chunk, group * GROUP + lax.rem(my_seat + t, GROUP))
-                return inner2
-
-            lax.fori_loop(0, GROUP, one, 0)
+            post(1, send_b, got_b, chunk, group)
             return inner
 
         lax.fori_loop(0, GROUPS, backward, 0)
@@ -290,31 +277,28 @@
         return total
 
     def collect(chunk, sums):
-        def tile(step, sums):
-            group = group_of(step // 2)
-            g = 2 * group + lax.rem(step, 2)
-
-            @pl.when(lax.rem(step, 2) == 0)
-            def _():
-                arrived(1, send_b, got_b, chunk, group)
-
-            parts = [got_b[chunk, 4 * g + i].astype(jnp.float32) for i in range(4)]
-            outs = spread(parts, quarter)
-            at = pl.ds(pl.multiple_of(chunk * HALF + g * 128, 128), 128)
+        def tiles(step, sums):
+            group = group_of(step)
+            arrived(1, send_b, got_b, chunk, group)
             num_re, num_im, energy = sums
-            for h in range(2):
-                re, im = outs[2 * h], outs[2 * h + 1]
-                rows = slice(SUB * h, SUB * h + SUB)
-                mult[0, 0, rows, at] = re.astype(jnp.bfloat16)
-                mult[0, 1, rows, at] = im.astype(jnp.bfloat16)
-                data_re = rec[0, 0, rows, at]
-                data_im = rec[0, 1, rows, at]
-                num_re = num_re + fold(re * data_re + im * data_im)
-                num_im = num_im + fold(re * data_im - im * data_re)
-                energy = energy + fold(re * re + im * im)
+            for part in range(2):
+                g = 2 * group + part
+                parts = [got_b[chunk, 4 * g + i].astype(jnp.float32) for i in range(4)]
+                outs = spread(parts, quarter)
+                at = pl.ds(pl.multiple_of(chunk * HALF + g * 128, 128), 128)
+                for h in range(2):
+                    re, im = outs[2 * h], outs[2 * h + 1]
+                    rows = slice(SUB * h, SUB * h + SUB)
+                    mult[0, 0, rows, at] = re.astype(jnp.bfloat16)
+                    mult[0, 1, rows, at] = im.astype(jnp.bfloat16)
+                    data_re = rec[0, 0, rows, at]
+                    data_im = rec[0, 1, rows, at]
+                    num_re = num_re + fold(re * data_re + im * data_im)
+                    num_im = num_im + fold(re * data_im - im * data_re)
+                    energy = energy + fold(re * re + im * im)
             return num_re, num_im, energy
 
-        return lax.fori_loop(0, PANELS // 4, tile, sums)
+        return lax.fori_loop(0, GROUPS, tiles, sums)
 
     zero = jnp.zeros((8, 128), jnp.float32)
     sums = lax.fori_loop(0, CHUNKS, collect, (zero, zero, zero))
@@ -324,7 +308,7 @@
     part_out[0:1, 0:1] = mine[None]
     part_in[pl.ds(me, 1), 0:1] = mine[None]
 
-    def share(k, carry):
+    for k in range(1, PANELS):
         target = lax.rem(me + k, PANELS)
         pltpu.make_async_remote_copy(
             src_ref=part_out.at[pl.ds(0, 1), pl.ds(0, 1)],
@@ -334,9 +318,6 @@
             device_id={"panel": target},
             device_id_type=MESH,
         ).start()
-        return carry
-
-    lax.fori_loop(1, PANELS, share, 0)
     for chunk in range(CHUNKS):
         sent(0, send_a, got_a, chunk)
         sent(1, send_b, got_b, chunk)

time: 48.8 us -> 46.6 us (0.955)
  Pallas kernels: 48 us -> 45.8 us
    pallas_call x1, Pallas kernels: 46.8 us -> 44.6 us  [per_device(): pl.pallas_call(kernel, out_shape=(outs[1], outs[0], jax.ShapeDtypeStruct(...]
where the time goes in v6:
time: 46.6 us; the launch traced here: 46.4 us
  Pallas kernels  45.8 us (98%)
  between operations  0.64 us (1%)
    pallas_call x1, Pallas kernels, per_device(): pl.pallas_call(kernel, out_shape=(outs[1], outs[0], jax.ShapeDtypeStruct(...  44.6 us
    pallas_call x1, Pallas kernels, per_device(): pl.pallas_call(finish, out_shape=outs, in_specs=[pl.BlockSpec(memory_spac...  1.19 us

profile of v6, /device:TPU:1, one launch (start us, length us, event | category | flops | bytes accessed | tf_op | source)
XLA Modules:
  0.0 46.4 jit_solution(10541409505527838109)
XLA Ops:
  0.6 44.6 %shard_map.50 = (bf16[1,2,64,2048]{3,2,1,0:T(8,128)(2,1)S(1)}, f32[1,2,64,2048]{3,2,1,0:T(8,128)S(1)}, f32[8,128]{1,0:T(8,128)S(1)}) custom-call(f32[1,2,64,2048]{3,2,1,0:T(8,128)} %rec_hbm.1, bf16[1,2,4095]{2,1,0:T(2,128)(2,1)} %receiver_hbm.1, bf16[1,2,4095]{2,1,0:T(2,128)(2,1)} %source_hbm.1), custom_call_target="tpu_custom_call" | custom-call | tf_op jit(solution)/shard_map/pallas_call | solution.py:377
  45.2 1.2 %shard_map.51 = (f32[1,2,64,2048]{3,2,1,0:T(8,128)}, bf16[1,2,64,2048]{3,2,1,0:T(8,128)(2,1)}) custom-call(bf16[1,2,64,2048]{3,2,1,0:T(8,128)(2,1)S(1)} %get-tuple-element.5.mult, f32[1,2,64,2048]{3,2,1,0:T(8,128)S(1)} %get-tuple-element.6.rec, f32[8,128]{1,0:T(8,128)S(1)} %get-tuple-element.7.sums_ref), custom_call_target="tpu_custom_call" | custom-call | tf_op jit(solution)/shard_map/pallas_call | solution.py:406

commit v7 on v6

--- a/solution.py
+++ b/solution.py
@@ -122,7 +122,7 @@
             bulk(stage, src, dst, chunk, group, group * GROUP, GROUP - 1).wait_recv()
 
     def group_of(turn):
-        away = jnp.where(turn < 2, 2 * turn + 1, 6 - 2 * turn)
+        away = jnp.where(turn < 2, 2 * turn + 1, 2 * turn - 4)
         return lax.rem(my_group + away, GROUPS)
 
     def post(stage, src, dst, chunk, group):
@@ -145,9 +145,9 @@
     def build_receiver(index, carry):
         for e in range(8):
             rows = rolled_taps(taps_ref, index, e)
-            for u in range(UNITS):
-                at = 128 * (UNITS - 1 - u)
-                oper[index, 128 * u + 16 * e : 128 * u + 16 * e + 16, :] = rows[:, at : at + 256]
+            for u in range(UNITS + 1):
+                at = 128 * (UNITS - u)
+                oper[index, 128 * u + 16 * e : 128 * u + 16 * e + 16, :] = rows[:, at : at + 128]
         return carry
 
     lax.fori_loop(0, 2, build_receiver, 0)
@@ -164,11 +164,12 @@
         chunk = step // GROUPS
         group = group_of(lax.rem(step, GROUPS))
         at = pl.multiple_of((BLOCKS - 1 - chunk * GROUPS - group) * BLOCK, BLOCK)
-        result = jnp.dot(
-            left[...], oper[0, pl.ds(at, WIDTH), :], preferred_element_type=jnp.float32
-        ) + jnp.dot(
-            left_turned[...], oper[1, pl.ds(at, WIDTH), :], preferred_element_type=jnp.float32
-        )
+        terms = []
+        for index, lhs in enumerate((left, left_turned)):
+            halves = [oper[index, pl.ds(at + 128, WIDTH), :], oper[index, pl.ds(at, WIDTH), :]]
+            rhs = jnp.concatenate(halves, axis=1)
+            terms.append(jnp.dot(lhs[...], rhs, preferred_element_type=jnp.float32))
+        result = terms[0] + terms[1]
         for g in range(2):
             lanes = slice(128 * g, 128 * g + 128)
             parts = [
@@ -382,7 +383,7 @@
         scratch_shapes=[
             vmem((2, 2, TAPS - 1), bf16),
             vmem((16, TAPS), jnp.float32),
-            vmem((2, 128 * UNITS, BLOCK), bf16),
+            vmem((2, 128 * (UNITS + 1), 128), bf16),
             vmem((128, TAPS), bf16),
             vmem((2, 128 * UNITS, BLOCK), bf16),
             vmem((2 * ROWS, WIDTH), bf16),

time: 46.6 us -> 46.3 us (level)
  no operation moved by 1% of the time
where the time goes in v7:
time: 46.3 us; the launch traced here: 46.1 us
  Pallas kernels  45.4 us (98%)
  between operations  0.64 us (1%)
    pallas_call x1, Pallas kernels, per_device(): pl.pallas_call(kernel, out_shape=(outs[1], outs[0], jax.ShapeDtypeStruct(...  44.3 us
    pallas_call x1, Pallas kernels, per_device(): pl.pallas_call(finish, out_shape=outs, in_specs=[pl.BlockSpec(memory_spac...  1.19 us

profile of v7, /device:TPU:1, one launch (start us, length us, event | category | flops | bytes accessed | tf_op | source)
XLA Modules:
  0.0 46.1 jit_solution(7454801988339004545)
XLA Ops:
  0.6 44.3 %shard_map.50 = (bf16[1,2,64,2048]{3,2,1,0:T(8,128)(2,1)S(1)}, f32[1,2,64,2048]{3,2,1,0:T(8,128)S(1)}, f32[8,128]{1,0:T(8,128)S(1)}) custom-call(f32[1,2,64,2048]{3,2,1,0:T(8,128)} %rec_hbm.1, bf16[1,2,4095]{2,1,0:T(2,128)(2,1)} %receiver_hbm.1, bf16[1,2,4095]{2,1,0:T(2,128)(2,1)} %source_hbm.1), custom_call_target="tpu_custom_call" | custom-call | tf_op jit(solution)/shard_map/pallas_call | solution.py:378
  44.9 1.2 %shard_map.51 = (f32[1,2,64,2048]{3,2,1,0:T(8,128)}, bf16[1,2,64,2048]{3,2,1,0:T(8,128)(2,1)}) custom-call(bf16[1,2,64,2048]{3,2,1,0:T(8,128)(2,1)S(1)} %get-tuple-element.5.mult, f32[1,2,64,2048]{3,2,1,0:T(8,128)S(1)} %get-tuple-element.6.rec, f32[8,128]{1,0:T(8,128)S(1)} %get-tuple-element.7.sums_ref), custom_call_target="tpu_custom_call" | custom-call | tf_op jit(solution)/shard_map/pallas_call | solution.py:407

commit v8 on v7

--- a/solution.py
+++ b/solution.py
@@ -122,7 +122,7 @@
             bulk(stage, src, dst, chunk, group, group * GROUP, GROUP - 1).wait_recv()
 
     def group_of(turn):
-        away = jnp.where(turn < 2, 2 * turn + 1, 2 * turn - 4)
+        away = jnp.where(turn < 2, 2 * turn + 1, 6 - 2 * turn)
         return lax.rem(my_group + away, GROUPS)
 
     def post(stage, src, dst, chunk, group):

time: 46.3 us -> 46.7 us (level)
  no operation moved by 1% of the time
where the time goes in v8:
time: 46.7 us; the launch traced here: 46.5 us
  Pallas kernels  45.8 us (98%)
  between operations  0.64 us (1%)
    pallas_call x1, Pallas kernels, per_device(): pl.pallas_call(kernel, out_shape=(outs[1], outs[0], jax.ShapeDtypeStruct(...  44.7 us
    pallas_call x1, Pallas kernels, per_device(): pl.pallas_call(finish, out_shape=outs, in_specs=[pl.BlockSpec(memory_spac...  1.19 us

profile of v8, /device:TPU:1, one launch (start us, length us, event | category | flops | bytes accessed | tf_op | source)
XLA Modules:
  0.0 46.5 jit_solution(5748011237310237829)
XLA Ops:
  0.6 44.7 %shard_map.50 = (bf16[1,2,64,2048]{3,2,1,0:T(8,128)(2,1)S(1)}, f32[1,2,64,2048]{3,2,1,0:T(8,128)S(1)}, f32[8,128]{1,0:T(8,128)S(1)}) custom-call(f32[1,2,64,2048]{3,2,1,0:T(8,128)} %rec_hbm.1, bf16[1,2,4095]{2,1,0:T(2,128)(2,1)} %receiver_hbm.1, bf16[1,2,4095]{2,1,0:T(2,128)(2,1)} %source_hbm.1), custom_call_target="tpu_custom_call" | custom-call | tf_op jit(solution)/shard_map/pallas_call | solution.py:378
  45.3 1.2 %shard_map.51 = (f32[1,2,64,2048]{3,2,1,0:T(8,128)}, bf16[1,2,64,2048]{3,2,1,0:T(8,128)(2,1)}) custom-call(bf16[1,2,64,2048]{3,2,1,0:T(8,128)(2,1)S(1)} %get-tuple-element.5.mult, f32[1,2,64,2048]{3,2,1,0:T(8,128)S(1)} %get-tuple-element.6.rec, f32[8,128]{1,0:T(8,128)S(1)} %get-tuple-element.7.sums_ref), custom_call_target="tpu_custom_call" | custom-call | tf_op jit(solution)/shard_map/pallas_call | solution.py:407
